TPU v7x, 32 devices: a whole 2x2x4 slice. The times are simulated.
32 devices in a mesh: dp: 2 (over x), cp: 16 (over z, y, core).
Axes of the slice: x: 2, y: 2, z: 4, core: 2. Of those that a mesh axis runs over, the one named last changes fastest.
Arguments:
- x: bfloat16 [8192, 4096], P(('dp', 'cp')), parts along dimension 0
- seg: int32 [8192], P(('dp', 'cp')), parts along dimension 0
- wq: bfloat16 [4096, 4096], replicated
- wk: bfloat16 [4096, 1024], replicated
- wv: bfloat16 [4096, 1024], replicated
- wo: bfloat16 [4096, 4096], replicated
Outputs:
- output: bfloat16 [8192, 4096], P(('dp', 'cp')), parts along dimension 0
There are 2 independent parts. A program takes and returns all parts, laid end to end along the dimension named above; an argument that names none is the same for every part.
All inputs are finite; a program needn't handle non-finite values.
Results may differ from a plain program's by a relative error of at most 0.00590055.
Values are sent between devices in bfloat16 or wider.
A program may use at most 1 GiB of HBM per device.

v0:
```python
import jax
import jax.numpy as jnp
from jax import lax
from jax.sharding import PartitionSpec as P

DH = 128


def _positions(src, n, half):
    ar = jnp.arange(half, dtype=jnp.int32)
    return jnp.concatenate([src * half + ar, (2 * n - 1 - src) * half + ar])


def _block(q, k, v, mask, m, l, acc):
    s = jnp.einsum("qhgd,khd->hgqk", q, k, preferred_element_type=jnp.float32) * (DH ** -0.5)
    s = jnp.where(mask, s, -jnp.inf)
    m_new = jnp.maximum(m, s.max(axis=-1))
    m_safe = jnp.where(jnp.isfinite(m_new), m_new, 0.0)
    p = jnp.exp(s - m_safe[..., None])
    corr = jnp.exp(m - m_safe)
    l = l * corr + p.sum(axis=-1)
    pv = jnp.einsum("hgqk,khd->qhgd", p.astype(jnp.bfloat16), v, preferred_element_type=jnp.float32)
    acc = acc * jnp.transpose(corr, (2, 0, 1))[..., None] + pv
    return m_new, l, acc


def _finish(l, acc, wo):
    o = (acc / jnp.transpose(l, (2, 0, 1))[..., None]).astype(jnp.bfloat16)
    o = o.reshape(o.shape[0], -1)
    return jnp.dot(o, wo, preferred_element_type=jnp.float32).astype(jnp.bfloat16)


def solution(mesh):
    n = mesh.shape["cp"]
    perm = [(j, (j + 1) % n) for j in range(n)]

    def local(x, seg, wq, wk, wv, wo):
        lq = x.shape[0]
        half = lq // 2
        hq = wq.shape[1] // DH
        hkvv = wk.shape[1] // DH
        g = hq // hkvv
        me = lax.axis_index("cp")
        pos = _positions(me, n, half)
        q = jnp.dot(x, wq, preferred_element_type=jnp.float32).astype(jnp.bfloat16).reshape(lq, hkvv, g, DH)
        k = jnp.dot(x, wk, preferred_element_type=jnp.float32).astype(jnp.bfloat16).reshape(lq, hkvv, DH)
        v = jnp.dot(x, wv, preferred_element_type=jnp.float32).astype(jnp.bfloat16).reshape(lq, hkvv, DH)
        m = jnp.full((hkvv, g, lq), -jnp.inf, jnp.float32)
        l = jnp.zeros((hkvv, g, lq), jnp.float32)
        acc = jnp.zeros((lq, hkvv, g, DH), jnp.float32)
        kb, vb, sb = k, v, seg
        for step in range(n):
            if step > 0:
                kb = lax.ppermute(kb, "cp", perm)
                vb = lax.ppermute(vb, "cp", perm)
                sb = lax.ppermute(sb, "cp", perm)
            src = (me - step) % n
            mask = (seg[:, None] == sb[None, :]) & (_positions(src, n, half)[None, :] <= pos[:, None])
            m, l, acc = _block(q, kb, vb, mask, m, l, acc)
        return _finish(l, acc, wo)

    rows = P(("dp", "cp"), None)
    return jax.shard_map(local, mesh=mesh, in_specs=(rows, P(("dp", "cp")), P(), P(), P(), P()), out_specs=rows, check_vma=False)
```

profile of v0, /device:TPU:5, one launch (start us, length us, event | category | flops | bytes accessed | tf_op | source)
XLA Modules:
  0.0 465.8 jit_solution(964054124457411392)
XLA Ops:
  1.8 6.5 %convolution_convert_fusion.3 = bf16[256,1024]{1,0:T(8,128)(2,1)S(1)} fusion(bf16[256,4096]{1,0:T(8,128)(2,1)S(1)} %copy-done, bf16[4096,1024]{1,0:T(8,128)(2,1)} %param.9), kind=kOutput, calls=%fused_computation.196 | convolution fusion | flops 2147745792 | bytes 11010048 | tf_op jit(solution)/shard_map/dot_general | solution.py:46
  14.5 16.6 %convolution_convert_fusion.1 = bf16[256,4096]{1,0:T(8,128)(2,1)} fusion(bf16[256,4096]{1,0:T(8,128)(2,1)S(1)} %copy-done, bf16[4096,4096]{1,0:T(8,128)(2,1)} %param.8), kind=kOutput, calls=%fused_computation.81 | convolution fusion | flops 8590983168 | bytes 37748736 | tf_op jit(solution)/shard_map/dot_general | solution.py:45
  33.1 5.9 %collective-permute-done.4 = bf16[256,8,128]{2,0,1:T(8,128)(2,1)S(1)} collective-permute-done((bf16[256,8,128]{2,0,1:T(8,128)(2,1)}, bf16[256,8,128]{2,0,1:T(8,128)(2,1)S(1)}, u32[]{:S(2)}, u32[]{:S(2)}) %collective-permute-start.4) | collective-permute-done | bytes 524320 | tf_op jit(solution)/shard_map/ppermute | solution.py:54
  59.3 7.7 %collective-permute-done.3 = s32[256]{0:T(256)S(1)} collective-permute-done((s32[256]{0:T(256)S(1)}, s32[256]{0:T(256)S(1)}, u32[]{:S(2)}, u32[]{:S(2)}) %collective-permute-start.3) | collective-permute-done | bytes 1056 | tf_op jit(solution)/shard_map/ppermute | solution.py:56
  126.0 5.4 %fusion.32 = (f32[8,4,256]{2,1,0:T(4,128)S(1)}, f32[8,256,256,4]{2,1,3,0:T(8,128)}) fusion(pred[256,256]{0,1:T(8,128)(4,1)S(1)} %get-tuple-element.58, bf16[256,8,4,128]{3,2,1,0:T(4,128)(2,1)S(1)} %reshape.383, bf16[256,8,128,1]{2,1,0,3:T(8,128)(2,1)S(1)} %bitcast.666), kind=kOutput, calls=%fused_computation.64 | convolution fusion | flops 543154176 | bytes 11108352 | tf_op jit(solution)/shard_map/qhgd,khd->hgqk/dot_general | solution.py:15
  141.1 5.3 %fusion.34 = (f32[8,4,256]{2,1,0:T(4,128)S(1)}, f32[8,256,256,4]{2,1,3,0:T(8,128)}) fusion(pred[256,256]{0,1:T(8,128)(4,1)S(1)} %get-tuple-element.51, bf16[256,8,4,128]{3,2,1,0:T(4,128)(2,1)S(1)} %reshape.383, bf16[256,8,128]{2,0,1:T(8,128)(2,1)S(1)} %copy-done.9), kind=kOutput, calls=%fused_computation.66 | convolution fusion | flops 543154176 | bytes 11108352 | tf_op jit(solution)/shard_map/qhgd,khd->hgqk/dot_general | solution.py:15
  147.1 5.3 %fusion.35 = (f32[8,4,256]{2,1,0:T(4,128)S(1)}, f32[8,256,256,4]{2,1,3,0:T(8,128)}) fusion(pred[256,256]{0,1:T(8,128)(4,1)S(1)} %get-tuple-element.52, bf16[256,8,4,128]{3,2,1,0:T(4,128)(2,1)S(1)} %reshape.383, bf16[256,8,128]{2,0,1:T(8,128)(2,1)S(1)} %copy-done.11), kind=kOutput, calls=%fused_computation.67 | convolution fusion | flops 543154176 | bytes 11108352 | tf_op jit(solution)/shard_map/qhgd,khd->hgqk/dot_general | solution.py:15
  153.8 6.4 %fusion.36 = (f32[8,4,256]{2,1,0:T(4,128)S(1)}, f32[8,256,256,4]{2,1,3,0:T(8,128)}) fusion(pred[256,256]{0,1:T(8,128)(4,1)S(1)} %get-tuple-element.53, bf16[256,8,4,128]{3,2,1,0:T(4,128)(2,1)S(1)} %reshape.383, bf16[256,8,128]{2,0,1:T(8,128)(2,1)} %collective-permute-done.10), kind=kOutput, calls=%fused_computation.68 | convolution fusion | flops 543154176 | bytes 11108352 | tf_op jit(solution)/shard_map/qhgd,khd->hgqk/dot_general | solution.py:15
  162.5 6.3 %fusion.37 = (f32[8,4,256]{2,1,0:T(4,128)S(1)}, f32[8,256,256,4]{2,1,3,0:T(8,128)}) fusion(pred[256,256]{0,1:T(8,128)(4,1)S(1)} %get-tuple-element.54, bf16[256,8,4,128]{3,2,1,0:T(4,128)(2,1)S(1)} %reshape.383, bf16[256,8,128]{2,0,1:T(8,128)(2,1)} %collective-permute-done.13), kind=kOutput, calls=%fused_computation.69 | convolution fusion | flops 543154176 | bytes 11108352 | tf_op jit(solution)/shard_map/qhgd,khd->hgqk/dot_general | solution.py:15
  171.7 6.4 %fusion.38 = (f32[8,4,256]{2,1,0:T(4,128)S(1)}, f32[8,256,256,4]{2,1,3,0:T(8,128)}) fusion(pred[256,256]{0,1:T(8,128)(4,1)S(1)} %get-tuple-element.55, bf16[256,8,4,128]{3,2,1,0:T(4,128)(2,1)S(1)} %reshape.383, bf16[256,8,128]{2,0,1:T(8,128)(2,1)} %collective-permute-done.16), kind=kOutput, calls=%fused_computation.70 | convolution fusion | flops 543154176 | bytes 11108352 | tf_op jit(solution)/shard_map/qhgd,khd->hgqk/dot_general | solution.py:15
  178.1 5.0 %collective-permute-start.32 = (bf16[256,8,128]{0,2,1:T(8,128)(2,1)S(1)}, bf16[256,8,128]{0,2,1:T(8,128)(2,1)S(1)}, u32[]{:S(2)}, u32[]{:S(2)}) collective-permute-start(bf16[256,8,128]{0,2,1:T(8,128)(2,1)S(1)} %collective-permute-done.29), channel_id=1, source_target_pairs={{0,1},{1,2},{2,3},{3,4},{4,5},{5,6},{6,7},{7,8},{8,9},{9,10},{10,1... | collective-permute-start | bytes 1572872 | tf_op jit(solution)/shard_map/ppermute | solution.py:55
  183.1 5.4 %fusion.39 = (f32[8,4,256]{2,1,0:T(4,128)S(1)}, f32[8,256,256,4]{2,1,3,0:T(8,128)}) fusion(pred[256,256]{0,1:T(8,128)(4,1)S(1)} %get-tuple-element.56, bf16[256,8,4,128]{3,2,1,0:T(4,128)(2,1)S(1)} %reshape.383, bf16[256,8,128]{2,0,1:T(8,128)(2,1)S(1)} %collective-permute-done.19), kind=kOutput, calls=%fused_computation.71 | convolution fusion | flops 543154176 | bytes 11108352 | tf_op jit(solution)/shard_map/qhgd,khd->hgqk/dot_general | solution.py:15
  190.8 5.3 %fusion.40 = (f32[8,4,256]{2,1,0:T(4,128)S(1)}, f32[8,256,256,4]{2,1,3,0:T(8,128)}) fusion(pred[256,256]{0,1:T(8,128)(4,1)S(1)} %get-tuple-element.57, bf16[256,8,4,128]{3,2,1,0:T(4,128)(2,1)S(1)} %reshape.383, bf16[256,8,128]{2,0,1:T(8,128)(2,1)S(1)} %collective-permute-done.22), kind=kOutput, calls=%fused_computation.72 | convolution fusion | flops 543154176 | bytes 11108352 | tf_op jit(solution)/shard_map/qhgd,khd->hgqk/dot_general | solution.py:15
  197.2 5.3 %fusion.41 = (f32[8,4,256]{2,1,0:T(4,128)S(1)}, f32[8,256,256,4]{2,1,3,0:T(8,128)}) fusion(pred[256,256]{0,1:T(8,128)(4,1)S(1)} %get-tuple-element.59, bf16[256,8,4,128]{3,2,1,0:T(4,128)(2,1)S(1)} %reshape.383, bf16[256,8,128]{2,0,1:T(8,128)(2,1)S(1)} %collective-permute-done.25), kind=kOutput, calls=%fused_computation.73 | convolution fusion | flops 543154176 | bytes 11108352 | tf_op jit(solution)/shard_map/qhgd,khd->hgqk/dot_general | solution.py:15
  206.3 5.3 %fusion.42 = (f32[8,4,256]{2,1,0:T(4,128)S(1)}, f32[8,256,256,4]{2,1,3,0:T(8,128)}) fusion(pred[256,256]{0,1:T(8,128)(4,1)S(1)} %get-tuple-element.60, bf16[256,8,4,128]{3,2,1,0:T(4,128)(2,1)S(1)} %reshape.383, bf16[256,8,128]{2,0,1:T(8,128)(2,1)S(1)} %collective-permute-done.28), kind=kOutput, calls=%fused_computation.74 | convolution fusion | flops 543154176 | bytes 11108352 | tf_op jit(solution)/shard_map/qhgd,khd->hgqk/dot_general | solution.py:15
  213.1 5.3 %fusion.43 = (f32[8,4,256]{2,1,0:T(4,128)S(1)}, f32[8,256,256,4]{2,1,3,0:T(8,128)}) fusion(pred[256,256]{0,1:T(8,128)(4,1)S(1)} %get-tuple-element.61, bf16[256,8,4,128]{3,2,1,0:T(4,128)(2,1)S(1)} %reshape.383, bf16[256,8,128]{2,0,1:T(8,128)(2,1)S(1)} %collective-permute-done.31), kind=kOutput, calls=%fused_computation.75 | convolution fusion | flops 543154176 | bytes 11108352 | tf_op jit(solution)/shard_map/qhgd,khd->hgqk/dot_general | solution.py:15
  221.0 5.3 %fusion.44 = (f32[8,4,256]{2,1,0:T(4,128)S(1)}, f32[8,256,256,4]{2,1,3,0:T(8,128)}) fusion(pred[256,256]{0,1:T(8,128)(4,1)S(1)} %get-tuple-element.62, bf16[256,8,4,128]{3,2,1,0:T(4,128)(2,1)S(1)} %reshape.383, bf16[256,8,128]{2,0,1:T(8,128)(2,1)S(1)} %collective-permute-done.34), kind=kOutput, calls=%fused_computation.76 | convolution fusion | flops 543154176 | bytes 11108352 | tf_op jit(solution)/shard_map/qhgd,khd->hgqk/dot_general | solution.py:15
  230.5 5.3 %fusion.45 = (f32[8,4,256]{2,1,0:T(4,128)S(1)}, f32[8,256,256,4]{2,1,3,0:T(8,128)}) fusion(pred[256,256]{0,1:T(8,128)(4,1)S(1)} %get-tuple-element.63, bf16[256,8,4,128]{3,2,1,0:T(4,128)(2,1)S(1)} %reshape.383, bf16[256,8,128]{2,0,1:T(8,128)(2,1)S(1)} %collective-permute-done.37), kind=kOutput, calls=%fused_computation.77 | convolution fusion | flops 543154176 | bytes 11108352 | tf_op jit(solution)/shard_map/qhgd,khd->hgqk/dot_general | solution.py:15
  237.4 5.3 %fusion.46 = (f32[8,4,256]{2,1,0:T(4,128)S(1)}, f32[8,256,256,4]{2,1,3,0:T(8,128)}) fusion(pred[256,256]{0,1:T(8,128)(4,1)S(1)} %get-tuple-element.64, bf16[256,8,4,128]{3,2,1,0:T(4,128)(2,1)S(1)} %reshape.383, bf16[256,8,128]{2,0,1:T(8,128)(2,1)S(1)} %collective-permute-done.40), kind=kOutput, calls=%fused_computation.78 | convolution fusion | flops 543154176 | bytes 11108352 | tf_op jit(solution)/shard_map/qhgd,khd->hgqk/dot_general | solution.py:15
  246.3 5.1 %fusion = f32[8,4,256]{2,1,0:T(4,128)S(1)} fusion(f32[8,256,256,4]{2,1,3,0:T(8,128)} %get-tuple-element.95, f32[8,4,256]{2,1,0:T(4,128)S(1)} %get-tuple-element.37, pred[256,256]{0,1:T(8,128)(4,1)S(1)} %get-tuple-element.58), kind=kLoop, calls=%fused_computation.32 | loop fusion | flops 8380416 | bytes 8519680 | tf_op jit(solution)/shard_map/reduce_sum | solution.py:21
  251.4 7.4 %fusion.78 = f32[8,128,4,256]{3,1,2,0:T(8,128)} fusion(f32[8,256,256,4]{2,1,3,0:T(8,128)} %get-tuple-element.95, f32[8,4,256]{2,1,0:T(4,128)S(1)} %get-tuple-element.37, pred[256,256]{0,1:T(8,128)(4,1)S(1)} %get-tuple-element.58, bf16[256,8,128,1]{2,1,0,3:T(8,128)(2,1)S(1)} %bitcast.664), kind=kOutput, calls=%fused_computation.97 | convolution fusion | flops 545259520 | bytes 13205504 | tf_op jit(solution)/shard_map/hgqk,khd->qhgd/dot_general | solution.py:22
  258.8 5.1 %fusion.16 = f32[8,4,256]{2,1,0:T(4,128)S(1)} fusion(f32[8,256,256,4]{2,1,3,0:T(8,128)} %get-tuple-element.81, f32[8,4,256]{2,1,0:T(4,128)S(1)} %get-tuple-element.43, pred[256,256]{0,1:T(8,128)(4,1)S(1)} %get-tuple-element.57), kind=kLoop, calls=%fused_computation.48 | loop fusion | flops 8380416 | bytes 8519680 | tf_op jit(solution)/shard_map/reduce_sum | solution.py:21
  263.9 5.1 %fusion.14 = f32[8,4,256]{2,1,0:T(4,128)S(1)} fusion(f32[8,256,256,4]{2,1,3,0:T(8,128)} %get-tuple-element.83, f32[8,4,256]{2,1,0:T(4,128)S(1)} %get-tuple-element.42, pred[256,256]{0,1:T(8,128)(4,1)S(1)} %get-tuple-element.56), kind=kLoop, calls=%fused_computation.46 | loop fusion | flops 8380416 | bytes 8519680 | tf_op jit(solution)/shard_map/reduce_sum | solution.py:21
  269.1 5.1 %fusion.12 = f32[8,4,256]{2,1,0:T(4,128)S(1)} fusion(f32[8,256,256,4]{2,1,3,0:T(8,128)} %get-tuple-element.85, f32[8,4,256]{2,1,0:T(4,128)S(1)} %get-tuple-element.41, pred[256,256]{0,1:T(8,128)(4,1)S(1)} %get-tuple-element.55), kind=kLoop, calls=%fused_computation.44 | loop fusion | flops 8380416 | bytes 8519680 | tf_op jit(solution)/shard_map/reduce_sum | solution.py:21
  274.2 5.1 %fusion.10 = f32[8,4,256]{2,1,0:T(4,128)S(1)} fusion(f32[8,256,256,4]{2,1,3,0:T(8,128)} %get-tuple-element.87, f32[8,4,256]{2,1,0:T(4,128)S(1)} %get-tuple-element.40, pred[256,256]{0,1:T(8,128)(4,1)S(1)} %get-tuple-element.54), kind=kLoop, calls=%fused_computation.42 | loop fusion | flops 8380416 | bytes 8519680 | tf_op jit(solution)/shard_map/reduce_sum | solution.py:21
  279.3 5.3 %fusion.8 = f32[8,4,256]{2,1,0:T(4,128)S(1)} fusion(f32[8,256,256,4]{2,1,3,0:T(8,128)} %get-tuple-element.89, f32[8,4,256]{2,1,0:T(4,128)S(1)} %get-tuple-element.39, pred[256,256]{0,1:T(8,128)(4,1)S(1)} %get-tuple-element.53), kind=kLoop, calls=%fused_computation.40 | loop fusion | flops 8380416 | bytes 8519680 | tf_op jit(solution)/shard_map/reduce_sum | solution.py:21
  284.7 5.1 %fusion.6 = f32[8,4,256]{2,1,0:T(4,128)S(1)} fusion(f32[8,256,256,4]{2,1,3,0:T(8,128)} %get-tuple-element.91, f32[8,4,256]{2,1,0:T(4,128)S(1)} %get-tuple-element.38, pred[256,256]{0,1:T(8,128)(4,1)S(1)} %get-tuple-element.52), kind=kLoop, calls=%fused_computation.38 | loop fusion | flops 8380416 | bytes 8519680 | tf_op jit(solution)/shard_map/reduce_sum | solution.py:21
  289.8 5.1 %fusion.20 = f32[8,4,256]{2,1,0:T(4,128)S(1)} fusion(f32[8,256,256,4]{2,1,3,0:T(8,128)} %get-tuple-element.77, f32[8,4,256]{2,1,0:T(4,128)S(1)} %get-tuple-element.45, pred[256,256]{0,1:T(8,128)(4,1)S(1)} %get-tuple-element.60), kind=kLoop, calls=%fused_computation.52 | loop fusion | flops 8380416 | bytes 8519680 | tf_op jit(solution)/shard_map/reduce_sum | solution.py:21
  294.9 5.1 %fusion.18 = f32[8,4,256]{2,1,0:T(4,128)S(1)} fusion(f32[8,256,256,4]{2,1,3,0:T(8,128)} %get-tuple-element.79, f32[8,4,256]{2,1,0:T(4,128)S(1)} %get-tuple-element.44, pred[256,256]{0,1:T(8,128)(4,1)S(1)} %get-tuple-element.59), kind=kLoop, calls=%fused_computation.50 | loop fusion | flops 8380416 | bytes 8519680 | tf_op jit(solution)/shard_map/reduce_sum | solution.py:21
  300.0 5.1 %fusion.24 = f32[8,4,256]{2,1,0:T(4,128)S(1)} fusion(f32[8,256,256,4]{2,1,3,0:T(8,128)} %get-tuple-element.73, f32[8,4,256]{2,1,0:T(4,128)S(1)} %get-tuple-element.47, pred[256,256]{0,1:T(8,128)(4,1)S(1)} %get-tuple-element.62), kind=kLoop, calls=%fused_computation.56 | loop fusion | flops 8380416 | bytes 8519680 | tf_op jit(solution)/shard_map/reduce_sum | solution.py:21
  305.2 5.1 %fusion.22 = f32[8,4,256]{2,1,0:T(4,128)S(1)} fusion(f32[8,256,256,4]{2,1,3,0:T(8,128)} %get-tuple-element.75, f32[8,4,256]{2,1,0:T(4,128)S(1)} %get-tuple-element.46, pred[256,256]{0,1:T(8,128)(4,1)S(1)} %get-tuple-element.61), kind=kLoop, calls=%fused_computation.54 | loop fusion | flops 8380416 | bytes 8519680 | tf_op jit(solution)/shard_map/reduce_sum | solution.py:21
  312.5 5.1 %fusion.28 = f32[8,4,256]{2,1,0:T(4,128)S(1)} fusion(f32[8,256,256,4]{2,1,3,0:T(8,128)} %get-tuple-element.69, f32[8,4,256]{2,1,0:T(4,128)S(1)} %get-tuple-element.49, pred[256,256]{0,1:T(8,128)(4,1)S(1)} %get-tuple-element.64), kind=kLoop, calls=%fused_computation.60 | loop fusion | flops 8380416 | bytes 8519680 | tf_op jit(solution)/shard_map/reduce_sum | solution.py:21
  317.6 5.1 %fusion.4 = f32[8,4,256]{2,1,0:T(4,128)S(1)} fusion(f32[8,256,256,4]{2,1,3,0:T(8,128)} %get-tuple-element.93, f32[8,4,256]{2,1,0:T(4,128)S(1)} %get-tuple-element.34, pred[256,256]{0,1:T(8,128)(4,1)S(1)} %get-tuple-element.51), kind=kLoop, calls=%fused_computation.36 | loop fusion | flops 8380416 | bytes 8519680 | tf_op jit(solution)/shard_map/reduce_sum | solution.py:21
  322.7 5.1 %fusion.26 = f32[8,4,256]{2,1,0:T(4,128)S(1)} fusion(f32[8,256,256,4]{2,1,3,0:T(8,128)} %get-tuple-element.71, f32[8,4,256]{2,1,0:T(4,128)S(1)} %get-tuple-element.48, pred[256,256]{0,1:T(8,128)(4,1)S(1)} %get-tuple-element.63), kind=kLoop, calls=%fused_computation.58 | loop fusion | flops 8380416 | bytes 8519680 | tf_op jit(solution)/shard_map/reduce_sum | solution.py:21
  330.1 7.6 %fusion.68 = f32[8,128,4,256]{3,1,2,0:T(8,128)} fusion(f32[8,256,256,4]{2,1,3,0:T(8,128)} %get-tuple-element.87, f32[8,4,256]{2,1,0:T(4,128)S(1)} %get-tuple-element.40, pred[256,256]{0,1:T(8,128)(4,1)S(1)} %get-tuple-element.54, bf16[256,8,128]{0,2,1:T(8,128)(2,1)} %collective-permute-done.14), kind=kOutput, calls=%fused_computation.92 | convolution fusion | flops 545259520 | bytes 13205504 | tf_op jit(solution)/shard_map/hgqk,khd->qhgd/dot_general | solution.py:22
  337.7 7.6 %fusion.70 = f32[8,128,4,256]{3,1,2,0:T(8,128)} fusion(f32[8,256,256,4]{2,1,3,0:T(8,128)} %get-tuple-element.89, f32[8,4,256]{2,1,0:T(4,128)S(1)} %get-tuple-element.39, pred[256,256]{0,1:T(8,128)(4,1)S(1)} %get-tuple-element.53, bf16[256,8,128]{0,2,1:T(8,128)(2,1)S(1)} %copy-done.7), kind=kOutput, calls=%fused_computation.93 | convolution fusion | flops 545259520 | bytes 13205504 | tf_op jit(solution)/shard_map/hgqk,khd->qhgd/dot_general | solution.py:22
  345.2 7.6 %fusion.72 = f32[8,128,4,256]{3,1,2,0:T(8,128)} fusion(f32[8,256,256,4]{2,1,3,0:T(8,128)} %get-tuple-element.91, f32[8,4,256]{2,1,0:T(4,128)S(1)} %get-tuple-element.38, pred[256,256]{0,1:T(8,128)(4,1)S(1)} %get-tuple-element.52, bf16[256,8,128]{0,2,1:T(8,128)(2,1)S(1)} %copy-done.5), kind=kOutput, calls=%fused_computation.94 | convolution fusion | flops 545259520 | bytes 13205504 | tf_op jit(solution)/shard_map/hgqk,khd->qhgd/dot_general | solution.py:22
  352.8 7.6 %fusion.66 = f32[8,128,4,256]{3,1,2,0:T(8,128)} fusion(f32[8,256,256,4]{2,1,3,0:T(8,128)} %get-tuple-element.85, f32[8,4,256]{2,1,0:T(4,128)S(1)} %get-tuple-element.41, pred[256,256]{0,1:T(8,128)(4,1)S(1)} %get-tuple-element.55, bf16[256,8,128]{0,2,1:T(8,128)(2,1)} %collective-permute-done.17), kind=kOutput, calls=%fused_computation.91 | convolution fusion | flops 545259520 | bytes 13205504 | tf_op jit(solution)/shard_map/hgqk,khd->qhgd/dot_general | solution.py:22
  360.4 7.4 %fusion.64 = f32[8,128,4,256]{3,1,2,0:T(8,128)} fusion(f32[8,256,256,4]{2,1,3,0:T(8,128)} %get-tuple-element.83, f32[8,4,256]{2,1,0:T(4,128)S(1)} %get-tuple-element.42, pred[256,256]{0,1:T(8,128)(4,1)S(1)} %get-tuple-element.56, bf16[256,8,128]{0,2,1:T(8,128)(2,1)S(1)} %collective-permute-done.20), kind=kOutput, calls=%fused_computation.90 | convolution fusion | flops 545259520 | bytes 13205504 | tf_op jit(solution)/shard_map/hgqk,khd->qhgd/dot_general | solution.py:22
  367.8 7.4 %fusion.62 = f32[8,128,4,256]{3,1,2,0:T(8,128)} fusion(f32[8,256,256,4]{2,1,3,0:T(8,128)} %get-tuple-element.81, f32[8,4,256]{2,1,0:T(4,128)S(1)} %get-tuple-element.43, pred[256,256]{0,1:T(8,128)(4,1)S(1)} %get-tuple-element.57, bf16[256,8,128]{0,2,1:T(8,128)(2,1)S(1)} %collective-permute-done.23), kind=kOutput, calls=%fused_computation.89 | convolution fusion | flops 545259520 | bytes 13205504 | tf_op jit(solution)/shard_map/hgqk,khd->qhgd/dot_general | solution.py:22
  375.2 7.4 %fusion.60 = f32[8,128,4,256]{3,1,2,0:T(8,128)} fusion(f32[8,256,256,4]{2,1,3,0:T(8,128)} %get-tuple-element.79, f32[8,4,256]{2,1,0:T(4,128)S(1)} %get-tuple-element.44, pred[256,256]{0,1:T(8,128)(4,1)S(1)} %get-tuple-element.59, bf16[256,8,128]{0,2,1:T(8,128)(2,1)S(1)} %collective-permute-done.26), kind=kOutput, calls=%fused_computation.88 | convolution fusion | flops 545259520 | bytes 13205504 | tf_op jit(solution)/shard_map/hgqk,khd->qhgd/dot_general | solution.py:22
  382.7 7.5 %fusion.58 = f32[8,128,4,256]{3,1,2,0:T(8,128)} fusion(f32[8,256,256,4]{2,1,3,0:T(8,128)} %get-tuple-element.77, f32[8,4,256]{2,1,0:T(4,128)S(1)} %get-tuple-element.45, pred[256,256]{0,1:T(8,128)(4,1)S(1)} %get-tuple-element.60, bf16[256,8,128]{0,2,1:T(8,128)(2,1)S(1)} %collective-permute-done.29), kind=kOutput, calls=%fused_computation.87 | convolution fusion | flops 545259520 | bytes 13205504 | tf_op jit(solution)/shard_map/hgqk,khd->qhgd/dot_general | solution.py:22
  390.2 7.6 %fusion.74 = f32[8,128,4,256]{3,1,2,0:T(8,128)} fusion(f32[8,256,256,4]{2,1,3,0:T(8,128)} %get-tuple-element.93, f32[8,4,256]{2,1,0:T(4,128)S(1)} %get-tuple-element.34, pred[256,256]{0,1:T(8,128)(4,1)S(1)} %get-tuple-element.51, bf16[256,8,128]{0,2,1:T(8,128)(2,1)S(1)} %copy-done.3), kind=kOutput, calls=%fused_computation.95 | convolution fusion | flops 545259520 | bytes 13205504 | tf_op jit(solution)/shard_map/hgqk,khd->qhgd/dot_general | solution.py:22
  397.7 5.3 %fusion.76 = f32[8,128,4,256]{3,1,2,0:T(8,128)} fusion(f32[8,256,256,4]{2,1,3,0:T(8,128)S(1)} %get-tuple-element.97, f32[8,4,256]{2,1,0:T(4,128)S(1)} %get-tuple-element.35, pred[256,256]{0,1:T(8,128)(4,1)S(1)} %get-tuple-element.50, bf16[256,8,128]{0,2,1:T(8,128)(2,1)} %collective-permute-done.2), kind=kOutput, calls=%fused_computation.96 | convolution fusion | flops 545259520 | bytes 13205504 | tf_op jit(solution)/shard_map/hgqk,khd->qhgd/dot_general | solution.py:22
  403.1 7.6 %fusion.56 = f32[8,128,4,256]{3,1,2,0:T(8,128)} fusion(f32[8,256,256,4]{2,1,3,0:T(8,128)} %get-tuple-element.75, f32[8,4,256]{2,1,0:T(4,128)S(1)} %get-tuple-element.46, pred[256,256]{0,1:T(8,128)(4,1)S(1)} %get-tuple-element.61, bf16[256,8,128]{0,2,1:T(8,128)(2,1)S(1)} %collective-permute-done.32), kind=kOutput, calls=%fused_computation.86 | convolution fusion | flops 545259520 | bytes 13205504 | tf_op jit(solution)/shard_map/hgqk,khd->qhgd/dot_general | solution.py:22
  418.8 7.5 %fusion.50 = f32[8,128,4,256]{3,1,2,0:T(8,128)} fusion(f32[8,256,256,4]{2,1,3,0:T(8,128)} %get-tuple-element.69, f32[8,4,256]{2,1,0:T(4,128)S(1)} %get-tuple-element.49, pred[256,256]{0,1:T(8,128)(4,1)S(1)} %get-tuple-element.64, bf16[256,8,128]{0,2,1:T(8,128)(2,1)S(1)} %collective-permute-done.41), kind=kOutput, calls=%fused_computation.83 | convolution fusion | flops 545259520 | bytes 13205504 | tf_op jit(solution)/shard_map/hgqk,khd->qhgd/dot_general | solution.py:22
  426.3 21.9 %fusion.81 = bf16[256,8,4,128]{0,3,2,1:T(8,128)(2,1)S(1)} fusion(f32[8,128,4,256]{3,1,2,0:T(8,128)} %fusion.50, f32[8,128,4,256]{3,1,2,0:T(8,128)} %fusion.52, f32[8,128,4,256]{3,1,2,0:T(8,128)} %fusion.54, f32[8,128,4,256]{3,1,2,0:T(8,128)} %fusion.56, f32[8,128,4,256]{3,1,2,0:T(8,128)} %fusion.58, f32[8,128,4,256]{3,1,2,0:T(8,128)} %fusion.60, ...), kind=kOutput, calls=%fused_computation.100 | convolution fusion | flops 579862528 | bytes 74579968 | tf_op jit(solution)/shard_map/hgqk,khd->qhgd/dot_general | solution.py:22
  448.3 17.1 %convolution_convert_fusion = bf16[256,4096]{1,0:T(8,128)(2,1)} fusion(bf16[256,4096]{0,1:T(8,128)(2,1)S(1)} %bitcast.662, bf16[4096,4096]{1,0:T(8,128)(2,1)} %param.11), kind=kOutput, calls=%fused_computation.80 | convolution fusion | flops 8590983168 | bytes 37748736 | tf_op jit(solution)/shard_map/dot_general | solution.py:30
  (182 shorter events, 139.1 us)
Async XLA Ops:
  0.0 59.2 %collective-permute-start = (s32[256]{0:T(256)}, s32[256]{0:T(256)S(1)}, u32[]{:S(2)}, u32[]{:S(2)}) collective-permute-start(s32[256]{0:T(256)} %param.7), channel_id=1, source_target_pairs={{0,1},{1,2},{2,3},{3,4},{4,5},{5,6},{6,7},{7,8},{8,9},{9,10},{10,1... | collective-permute-start | bytes 3080 | tf_op jit(solution)/shard_map/ppermute | solution.py:56
  9.2 22.1 %collective-permute-start.1 = (bf16[256,8,128]{2,0,1:T(8,128)(2,1)}, bf16[256,8,128]{2,0,1:T(8,128)(2,1)}, u32[]{:S(2)}, u32[]{:S(2)}) collective-permute-start(bf16[256,8,128]{2,0,1:T(8,128)(2,1)} %copy_bitcast_fusion), channel_id=1, source_target_pairs={{0,1},{1,2},{2,3},{3,4},{4,5},{5,6},{6,7},{7,8},{8,9},{9,10},{10,1... | collective-permute-start | bytes 1572872 | tf_op jit(solution)/shard_map/ppermute | solution.py:54
  14.4 18.5 %collective-permute-start.2 = (bf16[256,8,128]{0,2,1:T(8,128)(2,1)}, bf16[256,8,128]{0,2,1:T(8,128)(2,1)}, u32[]{:S(2)}, u32[]{:S(2)}) collective-permute-start(bf16[256,8,128]{0,2,1:T(8,128)(2,1)} %copy.13), channel_id=1, source_target_pairs={{0,1},{1,2},{2,3},{3,4},{4,5},{5,6},{6,7},{7,8},{8,9},{9,10},{10,1... | collective-permute-start | bytes 1572872 | tf_op jit(solution)/shard_map/ppermute | solution.py:55
  14.5 105.9 %copy-start.12 = (s32[256]{0:T(256)S(1)}, s32[256]{0:T(256)}, u32[]{:S(2)}) copy-start(s32[256]{0:T(256)} %param.7) | copy-start | bytes 3076
  31.3 7.7 %collective-permute-start.4 = (bf16[256,8,128]{2,0,1:T(8,128)(2,1)}, bf16[256,8,128]{2,0,1:T(8,128)(2,1)S(1)}, u32[]{:S(2)}, u32[]{:S(2)}) collective-permute-start(bf16[256,8,128]{2,0,1:T(8,128)(2,1)} %collective-permute-done.1), channel_id=1, source_target_pairs={{0,1},{1,2},{2,3},{3,4},{4,5},{5,6},{6,7},{7,8},{8,9},{9,10},{10,1... | collective-permute-start | bytes 1572872 | tf_op jit(solution)/shard_map/ppermute | solution.py:54
  32.9 11.7 %collective-permute-start.5 = (bf16[256,8,128]{0,2,1:T(8,128)(2,1)}, bf16[256,8,128]{0,2,1:T(8,128)(2,1)S(1)}, u32[]{:S(2)}, u32[]{:S(2)}) collective-permute-start(bf16[256,8,128]{0,2,1:T(8,128)(2,1)} %collective-permute-done.2), channel_id=1, source_target_pairs={{0,1},{1,2},{2,3},{3,4},{4,5},{5,6},{6,7},{7,8},{8,9},{9,10},{10,1... | collective-permute-start | bytes 1572872 | tf_op jit(solution)/shard_map/ppermute | solution.py:55
  39.0 11.2 %collective-permute-start.7 = (bf16[256,8,128]{2,0,1:T(8,128)(2,1)S(1)}, bf16[256,8,128]{2,0,1:T(8,128)(2,1)S(1)}, u32[]{:S(2)}, u32[]{:S(2)}) collective-permute-start(bf16[256,8,128]{2,0,1:T(8,128)(2,1)S(1)} %collective-permute-done.4), channel_id=1, source_target_pairs={{0,1},{1,2},{2,3},{3,4},{4,5},{5,6},{6,7},{7,8},{8,9},{9,10},{10,1... | collective-permute-start | bytes 1572872 | tf_op jit(solution)/shard_map/ppermute | solution.py:54
  44.6 71.9 %copy-start.2 = (bf16[256,8,128]{0,2,1:T(8,128)(2,1)}, bf16[256,8,128]{0,2,1:T(8,128)(2,1)S(1)}, u32[]{:S(2)}) copy-start(bf16[256,8,128]{0,2,1:T(8,128)(2,1)S(1)} %collective-permute-done.5) | copy-start | bytes 1572868
  44.6 11.2 %collective-permute-start.8 = (bf16[256,8,128]{0,2,1:T(8,128)(2,1)S(1)}, bf16[256,8,128]{0,2,1:T(8,128)(2,1)S(1)}, u32[]{:S(2)}, u32[]{:S(2)}) collective-permute-start(bf16[256,8,128]{0,2,1:T(8,128)(2,1)S(1)} %collective-permute-done.5), channel_id=1, source_target_pairs={{0,1},{1,2},{2,3},{3,4},{4,5},{5,6},{6,7},{7,8},{8,9},{9,10},{10,1... | collective-permute-start | bytes 1572872 | tf_op jit(solution)/shard_map/ppermute | solution.py:55
  50.2 66.3 %copy-start.10 = (bf16[256,8,128]{2,0,1:T(8,128)(2,1)}, bf16[256,8,128]{2,0,1:T(8,128)(2,1)S(1)}, u32[]{:S(2)}) copy-start(bf16[256,8,128]{2,0,1:T(8,128)(2,1)S(1)} %collective-permute-done.7) | copy-start | bytes 1572868
  50.2 24.2 %collective-permute-start.10 = (bf16[256,8,128]{2,0,1:T(8,128)(2,1)S(1)}, bf16[256,8,128]{2,0,1:T(8,128)(2,1)}, u32[]{:S(2)}, u32[]{:S(2)}) collective-permute-start(bf16[256,8,128]{2,0,1:T(8,128)(2,1)S(1)} %collective-permute-done.7), channel_id=1, source_target_pairs={{0,1},{1,2},{2,3},{3,4},{4,5},{5,6},{6,7},{7,8},{8,9},{9,10},{10,1... | collective-permute-start | bytes 1572872 | tf_op jit(solution)/shard_map/ppermute | solution.py:54
  55.8 28.1 %collective-permute-start.11 = (bf16[256,8,128]{0,2,1:T(8,128)(2,1)S(1)}, bf16[256,8,128]{0,2,1:T(8,128)(2,1)S(1)}, u32[]{:S(2)}, u32[]{:S(2)}) collective-permute-start(bf16[256,8,128]{0,2,1:T(8,128)(2,1)S(1)} %collective-permute-done.8), channel_id=1, source_target_pairs={{0,1},{1,2},{2,3},{3,4},{4,5},{5,6},{6,7},{7,8},{8,9},{9,10},{10,1... | collective-permute-start | bytes 1572872 | tf_op jit(solution)/shard_map/ppermute | solution.py:55
  59.2 7.8 %collective-permute-start.3 = (s32[256]{0:T(256)S(1)}, s32[256]{0:T(256)S(1)}, u32[]{:S(2)}, u32[]{:S(2)}) collective-permute-start(s32[256]{0:T(256)S(1)} %collective-permute-done), channel_id=1, source_target_pairs={{0,1},{1,2},{2,3},{3,4},{4,5},{5,6},{6,7},{7,8},{8,9},{9,10},{10,1... | collective-permute-start | bytes 3080 | tf_op jit(solution)/shard_map/ppermute | solution.py:56
  67.1 4.1 collective-permute-start.6
  71.2 3.9 collective-permute-start.9
  74.4 23.0 %collective-permute-start.13 = (bf16[256,8,128]{2,0,1:T(8,128)(2,1)}, bf16[256,8,128]{2,0,1:T(8,128)(2,1)}, u32[]{:S(2)}, u32[]{:S(2)}) collective-permute-start(bf16[256,8,128]{2,0,1:T(8,128)(2,1)} %collective-permute-done.10), channel_id=1, source_target_pairs={{0,1},{1,2},{2,3},{3,4},{4,5},{5,6},{6,7},{7,8},{8,9},{9,10},{10,1... | collective-permute-start | bytes 1572872 | tf_op jit(solution)/shard_map/ppermute | solution.py:54
  75.1 5.4 %collective-permute-start.12 = (s32[256]{0:T(256)S(1)}, s32[256]{0:T(256)S(1)}, u32[]{:S(2)}, u32[]{:S(2)}) collective-permute-start(s32[256]{0:T(256)S(1)} %collective-permute-done.9), channel_id=1, source_target_pairs={{0,1},{1,2},{2,3},{3,4},{4,5},{5,6},{6,7},{7,8},{8,9},{9,10},{10,1... | collective-permute-start | bytes 3080 | tf_op jit(solution)/shard_map/ppermute | solution.py:56
  80.5 4.1 collective-permute-start.15
  83.9 23.0 %collective-permute-start.14 = (bf16[256,8,128]{0,2,1:T(8,128)(2,1)S(1)}, bf16[256,8,128]{0,2,1:T(8,128)(2,1)}, u32[]{:S(2)}, u32[]{:S(2)}) collective-permute-start(bf16[256,8,128]{0,2,1:T(8,128)(2,1)S(1)} %collective-permute-done.11), channel_id=1, source_target_pairs={{0,1},{1,2},{2,3},{3,4},{4,5},{5,6},{6,7},{7,8},{8,9},{9,10},{10,1... | collective-permute-start | bytes 1572872 | tf_op jit(solution)/shard_map/ppermute | solution.py:55
  84.6 5.5 %collective-permute-start.18 = (s32[256]{0:T(256)S(1)}, s32[256]{0:T(256)S(1)}, u32[]{:S(2)}, u32[]{:S(2)}) collective-permute-start(s32[256]{0:T(256)S(1)} %collective-permute-done.15), channel_id=1, source_target_pairs={{0,1},{1,2},{2,3},{3,4},{4,5},{5,6},{6,7},{7,8},{8,9},{9,10},{10,1... | collective-permute-start | bytes 3080 | tf_op jit(solution)/shard_map/ppermute | solution.py:56
  90.1 4.1 collective-permute-start.21
  94.2 3.9 collective-permute-start.24
  97.4 23.0 %collective-permute-start.16 = (bf16[256,8,128]{2,0,1:T(8,128)(2,1)}, bf16[256,8,128]{2,0,1:T(8,128)(2,1)}, u32[]{:S(2)}, u32[]{:S(2)}) collective-permute-start(bf16[256,8,128]{2,0,1:T(8,128)(2,1)} %collective-permute-done.13), channel_id=1, source_target_pairs={{0,1},{1,2},{2,3},{3,4},{4,5},{5,6},{6,7},{7,8},{8,9},{9,10},{10,1... | collective-permute-start | bytes 1572872 | tf_op jit(solution)/shard_map/ppermute | solution.py:54
  98.1 5.4 %collective-permute-start.27 = (s32[256]{0:T(256)S(1)}, s32[256]{0:T(256)S(1)}, u32[]{:S(2)}, u32[]{:S(2)}) collective-permute-start(s32[256]{0:T(256)S(1)} %collective-permute-done.24), channel_id=1, source_target_pairs={{0,1},{1,2},{2,3},{3,4},{4,5},{5,6},{6,7},{7,8},{8,9},{9,10},{10,1... | collective-permute-start | bytes 3080 | tf_op jit(solution)/shard_map/ppermute | solution.py:56
  103.5 5.1 %collective-permute-start.30 = (s32[256]{0:T(256)S(1)}, s32[256]{0:T(256)S(1)}, u32[]{:S(2)}, u32[]{:S(2)}) collective-permute-start(s32[256]{0:T(256)S(1)} %collective-permute-done.27), channel_id=1, source_target_pairs={{0,1},{1,2},{2,3},{3,4},{4,5},{5,6},{6,7},{7,8},{8,9},{9,10},{10,1... | collective-permute-start | bytes 3080 | tf_op jit(solution)/shard_map/ppermute | solution.py:56
  106.9 18.8 %collective-permute-start.17 = (bf16[256,8,128]{0,2,1:T(8,128)(2,1)}, bf16[256,8,128]{0,2,1:T(8,128)(2,1)}, u32[]{:S(2)}, u32[]{:S(2)}) collective-permute-start(bf16[256,8,128]{0,2,1:T(8,128)(2,1)} %collective-permute-done.14), channel_id=1, source_target_pairs={{0,1},{1,2},{2,3},{3,4},{4,5},{5,6},{6,7},{7,8},{8,9},{9,10},{10,1... | collective-permute-start | bytes 1572872 | tf_op jit(solution)/shard_map/ppermute | solution.py:55
  108.7 5.7 %collective-permute-start.33 = (s32[256]{0:T(256)S(1)}, s32[256]{0:T(256)S(1)}, u32[]{:S(2)}, u32[]{:S(2)}) collective-permute-start(s32[256]{0:T(256)S(1)} %collective-permute-done.30), channel_id=1, source_target_pairs={{0,1},{1,2},{2,3},{3,4},{4,5},{5,6},{6,7},{7,8},{8,9},{9,10},{10,1... | collective-permute-start | bytes 3080 | tf_op jit(solution)/shard_map/ppermute | solution.py:56
  114.4 5.7 %collective-permute-start.36 = (s32[256]{0:T(256)S(1)}, s32[256]{0:T(256)S(1)}, u32[]{:S(2)}, u32[]{:S(2)}) collective-permute-start(s32[256]{0:T(256)S(1)} %collective-permute-done.33), channel_id=1, source_target_pairs={{0,1},{1,2},{2,3},{3,4},{4,5},{5,6},{6,7},{7,8},{8,9},{9,10},{10,1... | collective-permute-start | bytes 3080 | tf_op jit(solution)/shard_map/ppermute | solution.py:56
  120.1 5.7 %collective-permute-start.39 = (s32[256]{0:T(256)S(1)}, s32[256]{0:T(256)S(1)}, u32[]{:S(2)}, u32[]{:S(2)}) collective-permute-start(s32[256]{0:T(256)S(1)} %collective-permute-done.36), channel_id=1, source_target_pairs={{0,1},{1,2},{2,3},{3,4},{4,5},{5,6},{6,7},{7,8},{8,9},{9,10},{10,1... | collective-permute-start | bytes 3080 | tf_op jit(solution)/shard_map/ppermute | solution.py:56
  120.4 11.0 %collective-permute-start.19 = (bf16[256,8,128]{2,0,1:T(8,128)(2,1)}, bf16[256,8,128]{2,0,1:T(8,128)(2,1)S(1)}, u32[]{:S(2)}, u32[]{:S(2)}) collective-permute-start(bf16[256,8,128]{2,0,1:T(8,128)(2,1)} %collective-permute-done.16), channel_id=1, source_target_pairs={{0,1},{1,2},{2,3},{3,4},{4,5},{5,6},{6,7},{7,8},{8,9},{9,10},{10,1... | collective-permute-start | bytes 1572872 | tf_op jit(solution)/shard_map/ppermute | solution.py:54
  125.8 5.7 %collective-permute-start.42 = (s32[256]{0:T(256)S(1)}, s32[256]{0:T(256)S(1)}, u32[]{:S(2)}, u32[]{:S(2)}) collective-permute-start(s32[256]{0:T(256)S(1)} %collective-permute-done.39), channel_id=1, source_target_pairs={{0,1},{1,2},{2,3},{3,4},{4,5},{5,6},{6,7},{7,8},{8,9},{9,10},{10,1... | collective-permute-start | bytes 3080 | tf_op jit(solution)/shard_map/ppermute | solution.py:56
  125.8 6.6 %collective-permute-start.20 = (bf16[256,8,128]{0,2,1:T(8,128)(2,1)}, bf16[256,8,128]{0,2,1:T(8,128)(2,1)S(1)}, u32[]{:S(2)}, u32[]{:S(2)}) collective-permute-start(bf16[256,8,128]{0,2,1:T(8,128)(2,1)} %collective-permute-done.17), channel_id=1, source_target_pairs={{0,1},{1,2},{2,3},{3,4},{4,5},{5,6},{6,7},{7,8},{8,9},{9,10},{10,1... | collective-permute-start | bytes 1572872 | tf_op jit(solution)/shard_map/ppermute | solution.py:55
  131.4 8.4 %collective-permute-start.22 = (bf16[256,8,128]{2,0,1:T(8,128)(2,1)S(1)}, bf16[256,8,128]{2,0,1:T(8,128)(2,1)S(1)}, u32[]{:S(2)}, u32[]{:S(2)}) collective-permute-start(bf16[256,8,128]{2,0,1:T(8,128)(2,1)S(1)} %collective-permute-done.19), channel_id=1, source_target_pairs={{0,1},{1,2},{2,3},{3,4},{4,5},{5,6},{6,7},{7,8},{8,9},{9,10},{10,1... | collective-permute-start | bytes 1572872 | tf_op jit(solution)/shard_map/ppermute | solution.py:54
  132.4 14.0 %collective-permute-start.23 = (bf16[256,8,128]{0,2,1:T(8,128)(2,1)S(1)}, bf16[256,8,128]{0,2,1:T(8,128)(2,1)S(1)}, u32[]{:S(2)}, u32[]{:S(2)}) collective-permute-start(bf16[256,8,128]{0,2,1:T(8,128)(2,1)S(1)} %collective-permute-done.20), channel_id=1, source_target_pairs={{0,1},{1,2},{2,3},{3,4},{4,5},{5,6},{6,7},{7,8},{8,9},{9,10},{10,1... | collective-permute-start | bytes 1572872 | tf_op jit(solution)/shard_map/ppermute | solution.py:55
  139.8 12.6 %collective-permute-start.25 = (bf16[256,8,128]{2,0,1:T(8,128)(2,1)S(1)}, bf16[256,8,128]{2,0,1:T(8,128)(2,1)S(1)}, u32[]{:S(2)}, u32[]{:S(2)}) collective-permute-start(bf16[256,8,128]{2,0,1:T(8,128)(2,1)S(1)} %collective-permute-done.22), channel_id=1, source_target_pairs={{0,1},{1,2},{2,3},{3,4},{4,5},{5,6},{6,7},{7,8},{8,9},{9,10},{10,1... | collective-permute-start | bytes 1572872 | tf_op jit(solution)/shard_map/ppermute | solution.py:54
  146.5 13.8 %collective-permute-start.26 = (bf16[256,8,128]{0,2,1:T(8,128)(2,1)S(1)}, bf16[256,8,128]{0,2,1:T(8,128)(2,1)S(1)}, u32[]{:S(2)}, u32[]{:S(2)}) collective-permute-start(bf16[256,8,128]{0,2,1:T(8,128)(2,1)S(1)} %collective-permute-done.23), channel_id=1, source_target_pairs={{0,1},{1,2},{2,3},{3,4},{4,5},{5,6},{6,7},{7,8},{8,9},{9,10},{10,1... | collective-permute-start | bytes 1572872 | tf_op jit(solution)/shard_map/ppermute | solution.py:55
  152.4 16.5 %collective-permute-start.28 = (bf16[256,8,128]{2,0,1:T(8,128)(2,1)S(1)}, bf16[256,8,128]{2,0,1:T(8,128)(2,1)S(1)}, u32[]{:S(2)}, u32[]{:S(2)}) collective-permute-start(bf16[256,8,128]{2,0,1:T(8,128)(2,1)S(1)} %collective-permute-done.25), channel_id=1, source_target_pairs={{0,1},{1,2},{2,3},{3,4},{4,5},{5,6},{6,7},{7,8},{8,9},{9,10},{10,1... | collective-permute-start | bytes 1572872 | tf_op jit(solution)/shard_map/ppermute | solution.py:54
  160.2 17.9 %collective-permute-start.29 = (bf16[256,8,128]{0,2,1:T(8,128)(2,1)S(1)}, bf16[256,8,128]{0,2,1:T(8,128)(2,1)S(1)}, u32[]{:S(2)}, u32[]{:S(2)}) collective-permute-start(bf16[256,8,128]{0,2,1:T(8,128)(2,1)S(1)} %collective-permute-done.26), channel_id=1, source_target_pairs={{0,1},{1,2},{2,3},{3,4},{4,5},{5,6},{6,7},{7,8},{8,9},{9,10},{10,1... | collective-permute-start | bytes 1572872 | tf_op jit(solution)/shard_map/ppermute | solution.py:55
  168.9 19.6 %collective-permute-start.31 = (bf16[256,8,128]{2,0,1:T(8,128)(2,1)S(1)}, bf16[256,8,128]{2,0,1:T(8,128)(2,1)S(1)}, u32[]{:S(2)}, u32[]{:S(2)}) collective-permute-start(bf16[256,8,128]{2,0,1:T(8,128)(2,1)S(1)} %collective-permute-done.28), channel_id=1, source_target_pairs={{0,1},{1,2},{2,3},{3,4},{4,5},{5,6},{6,7},{7,8},{8,9},{9,10},{10,1... | collective-permute-start | bytes 1572872 | tf_op jit(solution)/shard_map/ppermute | solution.py:54
  178.1 18.0 %collective-permute-start.32 = (bf16[256,8,128]{0,2,1:T(8,128)(2,1)S(1)}, bf16[256,8,128]{0,2,1:T(8,128)(2,1)S(1)}, u32[]{:S(2)}, u32[]{:S(2)}) collective-permute-start(bf16[256,8,128]{0,2,1:T(8,128)(2,1)S(1)} %collective-permute-done.29), channel_id=1, source_target_pairs={{0,1},{1,2},{2,3},{3,4},{4,5},{5,6},{6,7},{7,8},{8,9},{9,10},{10,1... | collective-permute-start | bytes 1572872 | tf_op jit(solution)/shard_map/ppermute | solution.py:55
  188.5 14.1 %collective-permute-start.34 = (bf16[256,8,128]{2,0,1:T(8,128)(2,1)S(1)}, bf16[256,8,128]{2,0,1:T(8,128)(2,1)S(1)}, u32[]{:S(2)}, u32[]{:S(2)}) collective-permute-start(bf16[256,8,128]{2,0,1:T(8,128)(2,1)S(1)} %collective-permute-done.31), channel_id=1, source_target_pairs={{0,1},{1,2},{2,3},{3,4},{4,5},{5,6},{6,7},{7,8},{8,9},{9,10},{10,1... | collective-permute-start | bytes 1572872 | tf_op jit(solution)/shard_map/ppermute | solution.py:54
  196.1 15.5 %collective-permute-start.35 = (bf16[256,8,128]{0,2,1:T(8,128)(2,1)S(1)}, bf16[256,8,128]{0,2,1:T(8,128)(2,1)S(1)}, u32[]{:S(2)}, u32[]{:S(2)}) collective-permute-start(bf16[256,8,128]{0,2,1:T(8,128)(2,1)S(1)} %collective-permute-done.32), channel_id=1, source_target_pairs={{0,1},{1,2},{2,3},{3,4},{4,5},{5,6},{6,7},{7,8},{8,9},{9,10},{10,1... | collective-permute-start | bytes 1572872 | tf_op jit(solution)/shard_map/ppermute | solution.py:55
  202.5 15.9 %collective-permute-start.37 = (bf16[256,8,128]{2,0,1:T(8,128)(2,1)S(1)}, bf16[256,8,128]{2,0,1:T(8,128)(2,1)S(1)}, u32[]{:S(2)}, u32[]{:S(2)}) collective-permute-start(bf16[256,8,128]{2,0,1:T(8,128)(2,1)S(1)} %collective-permute-done.34), channel_id=1, source_target_pairs={{0,1},{1,2},{2,3},{3,4},{4,5},{5,6},{6,7},{7,8},{8,9},{9,10},{10,1... | collective-permute-start | bytes 1572872 | tf_op jit(solution)/shard_map/ppermute | solution.py:54
  211.6 14.7 %collective-permute-start.38 = (bf16[256,8,128]{0,2,1:T(8,128)(2,1)S(1)}, bf16[256,8,128]{0,2,1:T(8,128)(2,1)S(1)}, u32[]{:S(2)}, u32[]{:S(2)}) collective-permute-start(bf16[256,8,128]{0,2,1:T(8,128)(2,1)S(1)} %collective-permute-done.35), channel_id=1, source_target_pairs={{0,1},{1,2},{2,3},{3,4},{4,5},{5,6},{6,7},{7,8},{8,9},{9,10},{10,1... | collective-permute-start | bytes 1572872 | tf_op jit(solution)/shard_map/ppermute | solution.py:55
  218.4 9.6 %collective-permute-start.40 = (bf16[256,8,128]{2,0,1:T(8,128)(2,1)S(1)}, bf16[256,8,128]{2,0,1:T(8,128)(2,1)S(1)}, u32[]{:S(2)}, u32[]{:S(2)}) collective-permute-start(bf16[256,8,128]{2,0,1:T(8,128)(2,1)S(1)} %collective-permute-done.37), channel_id=1, source_target_pairs={{0,1},{1,2},{2,3},{3,4},{4,5},{5,6},{6,7},{7,8},{8,9},{9,10},{10,1... | collective-permute-start | bytes 1572872 | tf_op jit(solution)/shard_map/ppermute | solution.py:54
  226.3 9.5 %collective-permute-start.41 = (bf16[256,8,128]{0,2,1:T(8,128)(2,1)S(1)}, bf16[256,8,128]{0,2,1:T(8,128)(2,1)S(1)}, u32[]{:S(2)}, u32[]{:S(2)}) collective-permute-start(bf16[256,8,128]{0,2,1:T(8,128)(2,1)S(1)} %collective-permute-done.38), channel_id=1, source_target_pairs={{0,1},{1,2},{2,3},{3,4},{4,5},{5,6},{6,7},{7,8},{8,9},{9,10},{10,1... | collective-permute-start | bytes 1572872 | tf_op jit(solution)/shard_map/ppermute | solution.py:55
  228.0 14.8 %collective-permute-start.43 = (bf16[256,8,128]{2,0,1:T(8,128)(2,1)S(1)}, bf16[256,8,128]{2,0,1:T(8,128)(2,1)S(1)}, u32[]{:S(2)}, u32[]{:S(2)}) collective-permute-start(bf16[256,8,128]{2,0,1:T(8,128)(2,1)S(1)} %collective-permute-done.40), channel_id=1, source_target_pairs={{0,1},{1,2},{2,3},{3,4},{4,5},{5,6},{6,7},{7,8},{8,9},{9,10},{10,1... | collective-permute-start | bytes 1572872 | tf_op jit(solution)/shard_map/ppermute | solution.py:54
  235.8 190.5 %collective-permute-start.44 = (bf16[256,8,128]{0,2,1:T(8,128)(2,1)S(1)}, bf16[256,8,128]{0,2,1:T(8,128)(2,1)S(1)}, u32[]{:S(2)}, u32[]{:S(2)}) collective-permute-start(bf16[256,8,128]{0,2,1:T(8,128)(2,1)S(1)} %collective-permute-done.41), channel_id=1, source_target_pairs={{0,1},{1,2},{2,3},{3,4},{4,5},{5,6},{6,7},{7,8},{8,9},{9,10},{10,1... | collective-permute-start | bytes 1572872 | tf_op jit(solution)/shard_map/ppermute | solution.py:55
  (15 other events, 218.0 us)
where the time goes:
time: 475 us; the launch traced here: 466 us
  matrix products  253 us (53%)
  starting transfers between devices  86.9 us (18%)
  other arithmetic  78.4 us (17%)
  waiting for transfers between devices  40.8 us (9%)
  local copies, waits for them, and re-layouts  5.54 us (1%)
    dot_general x16, matrix products, _block(): jnp.einsum('hgqk,khd->qhgd', p.astype(jnp.bfloat16), v, preferred_element...  126 us
    dot_general x16, matrix products, _block(): jnp.einsum('qhgd,khd->hgqk', q, k, preferred_element_type=jnp.float32)  85.2 us
    reduce_sum x16, other arithmetic, _block(): l = l * corr + p.sum(axis=-1)  76 us
    ppermute x15, starting transfers between devices, local(): sb = lax.ppermute(sb, 'cp', perm)  35.9 us
    ppermute x15, waiting for transfers between devices, local(): sb = lax.ppermute(sb, 'cp', perm)  28 us
    ppermute x15, starting transfers between devices, local(): kb = lax.ppermute(kb, 'cp', perm)  26.8 us
    ppermute x15, starting transfers between devices, local(): vb = lax.ppermute(vb, 'cp', perm)  24.2 us
    dot_general x1, matrix products, _finish(): jnp.dot(o, wo, preferred_element_type=jnp.float32).astype(jnp.bfloat16)  17.1 us
  transfers between devices with their start and end apart: 45, of which 18 were waited for; matrix products, arithmetic and copies ran while one was open for 64% of the time, Pallas kernels for 0%

commit v1 on v0

v1 whole, which is shorter than its diff:
```python
import functools
import math

import jax
import jax.numpy as jnp
from jax import lax
from jax.experimental import pallas as pl
from jax.experimental.pallas import tpu as pltpu
from jax.sharding import PartitionSpec as P

DH = 128
NKV = 8
G = 4
PIECE = 128
CH = 4 * PIECE
SCALE = math.log2(math.e) / math.sqrt(DH)
NEG = -1e30


def _bias(segq_row, segk_rows, qp, kps):
    sq = jnp.transpose(jnp.broadcast_to(segq_row, (PIECE, PIECE)))
    rows = lax.broadcasted_iota(jnp.int32, (PIECE, PIECE), 0) + qp * PIECE
    lanes = lax.broadcasted_iota(jnp.int32, (PIECE, PIECE), 1)
    out = []
    for sk, kp in zip(segk_rows, kps):
        ok = (sq == sk) & (lanes + kp * PIECE <= rows)
        out.append(jnp.where(ok, 0.0, NEG))
    return jnp.concatenate(out, axis=1)


def _attn_kernel(q_ref, kv_ref, segq_ref, segk_ref, o_ref, bias_ref, m_ref, l_ref, acc_ref, *, me_fn):
    me = me_fn()
    z = me // 4
    h = pl.program_id(0)

    def chunk_of(step):
        lo = step <= z
        t = step - (z + 1)
        c_lo = jnp.where(step == 0, z, step - 1)
        c_hi = jnp.where(t == 0, 4 + z, jnp.where(t <= 4, t - 1, z + t))
        return lo, jnp.where(lo, c_lo, c_hi)

    @pl.when(h == 0)
    def _():
        def body(step, _):
            lo, c = chunk_of(step)
            qi = jnp.where(lo, 0, 1)
            qp = jnp.where(lo, me, 31 - me)
            hi = jnp.where(c >= 4, 1, 0)
            segk, kps = [], []
            for j in range(4):
                dev = 4 * (c - 4 * hi) + j
                segk.append(segk_ref[dev, pl.ds(hi, 1), :])
                kps.append(jnp.where(hi == 1, 31 - dev, dev))
            bias_ref[step] = _bias(segq_ref[pl.ds(qi, 1), :], segk, qp, kps)
            return 0
        lax.fori_loop(0, 9, body, 0)

    def piece(first, count, row0):
        m_ref[...] = jnp.full_like(m_ref, -jnp.inf)
        l_ref[...] = jnp.zeros_like(l_ref)
        acc_ref[...] = jnp.zeros_like(acc_ref)

        def body(i, _):
            step = first + i
            _, c = chunk_of(step)
            hi = jnp.where(c >= 4, 1, 0)
            dev = 4 * (c - 4 * hi)
            k = kv_ref[pl.ds(dev, 4), hi, 0, 0].reshape(CH, DH)
            v = kv_ref[pl.ds(dev, 4), hi, 0, 1].reshape(CH, DH)
            for g in range(G):
                q = q_ref[row0:row0 + PIECE, g * DH:(g + 1) * DH]
                s = lax.dot_general(q, k, (((1,), (1,)), ((), ())), preferred_element_type=jnp.float32)
                s = s * SCALE + bias_ref[step]
                m_old = m_ref[g]
                m_new = jnp.maximum(m_old, jnp.max(s, axis=1, keepdims=True))
                p = jnp.exp2(s - m_new[:, :1])
                corr = jnp.exp2(m_old - m_new)
                l_ref[g] = l_ref[g] * corr + jnp.sum(p, axis=1, keepdims=True)
                pv = lax.dot_general(p.astype(jnp.bfloat16), v, (((1,), (0,)), ((), ())), preferred_element_type=jnp.float32)
                acc_ref[g] = acc_ref[g] * corr + pv
                m_ref[g] = m_new
            return 0
        lax.fori_loop(0, count, body, 0)
        for g in range(G):
            o_ref[row0:row0 + PIECE, g * DH:(g + 1) * DH] = (acc_ref[g] / l_ref[g]).astype(jnp.bfloat16)

    piece(0, z + 1, 0)
    piece(z + 1, 8 - z, PIECE)


def solution(mesh):
    n = mesh.shape["cp"]

    def local(x, seg, wq, wk, wv, wo):
        k = jnp.dot(x, wk, preferred_element_type=jnp.float32).astype(jnp.bfloat16)
        v = jnp.dot(x, wv, preferred_element_type=jnp.float32).astype(jnp.bfloat16)
        kv = jnp.stack([k.reshape(2, PIECE, NKV, DH), v.reshape(2, PIECE, NKV, DH)], axis=0)
        kv = jnp.transpose(kv, (1, 3, 0, 2, 4))
        kv_all = lax.all_gather(kv, "cp", axis=0, tiled=False)
        segk = lax.all_gather(seg.reshape(2, PIECE), "cp", axis=0, tiled=False)
        q = jnp.dot(x, wq, preferred_element_type=jnp.float32).astype(jnp.bfloat16)
        o = pl.pallas_call(
            functools.partial(_attn_kernel, me_fn=lambda: lax.axis_index("cp")),
            out_shape=jax.ShapeDtypeStruct((2 * PIECE, NKV * G * DH), jnp.bfloat16),
            grid=(NKV,),
            in_specs=[
                pl.BlockSpec((2 * PIECE, G * DH), lambda h: (0, h)),
                pl.BlockSpec((n, 2, 1, 2, PIECE, DH), lambda h: (0, 0, h, 0, 0, 0)),
                pl.BlockSpec((2, PIECE), lambda h: (0, 0)),
                pl.BlockSpec((n, 2, PIECE), lambda h: (0, 0, 0)),
            ],
            out_specs=pl.BlockSpec((2 * PIECE, G * DH), lambda h: (0, h)),
            scratch_shapes=[
                pltpu.VMEM((9, PIECE, CH), jnp.float32),
                pltpu.VMEM((G, PIECE, DH), jnp.float32),
                pltpu.VMEM((G, PIECE, DH), jnp.float32),
                pltpu.VMEM((G, PIECE, DH), jnp.float32),
            ],
            cost_estimate=pl.CostEstimate(flops=10_000_000_000, bytes_accessed=20_000_000, transcendentals=0),
        )(q, kv_all, seg.reshape(2, PIECE), segk)
        return jnp.dot(o, wo, preferred_element_type=jnp.float32).astype(jnp.bfloat16)

    rows = P(("dp", "cp"), None)
    return jax.shard_map(local, mesh=mesh, in_specs=(rows, P(("dp", "cp")), P(), P(), P(), P()), out_specs=rows, check_vma=False)
```

time: 475 us -> 283 us (0.60)
  the two profiles are of different devices: /device:TPU:5 before, /device:TPU:27 now
where the time goes in v1:
time: 283 us; the launch traced here: 281 us
  Pallas kernels  113 us (40%)
  waiting for transfers between devices  91.7 us (32%)
  matrix products  41.7 us (15%)
  blocking collectives  17.6 us (6%)
  between operations  13.5 us (5%)
    pallas_call x1, Pallas kernels, local(): pl.pallas_call(functools.partial(_attn_kernel, me_fn=lambda: lax.axis_ind...  113 us
    all_gather x1, waiting for transfers between devices, local(): kv_all = lax.all_gather(kv, 'cp', axis=0, tiled=False)  91.7 us
    all_gather x1, blocking collectives, local(): segk = lax.all_gather(seg.reshape(2, PIECE), 'cp', axis=0, tiled=False)  17.6 us
    dot_general x1, matrix products, local(): jnp.dot(o, wo, preferred_element_type=jnp.float32).astype(jnp.bfloat16)  16.8 us
    dot_general x1, matrix products, local(): q = jnp.dot(x, wq, preferred_element_type=jnp.float32).astype(jnp.bfloat16)  16.6 us
    dot_general x1, matrix products, local(): k = jnp.dot(x, wk, preferred_element_type=jnp.float32).astype(jnp.bfloat16)  5.86 us
  transfers between devices with their start and end apart: 1, of which 1 were waited for; matrix products, arithmetic and copies ran while one was open for 6% of the time, Pallas kernels for 0%

profile of v1, /device:TPU:27, one launch (start us, length us, event | category | flops | bytes accessed | tf_op | source)
XLA Modules:
  0.0 280.6 jit_solution(10921410598397833790)
XLA Ops:
  6.5 0.0 copy-start
  6.5 0.0 all-gather.3.cloned.1.call-start
  6.5 1.6 copy-done
  8.1 0.0 copy-start.3
  8.1 5.9 %fusion = bf16[32,8,8,128]{3,1,2,0:T(8,128)(2,1)S(1)} fusion(bf16[256,4096]{1,0:T(8,128)(2,1)S(1)} %copy-done, bf16[4096,1024]{1,0:T(8,128)(2,1)} %param.9), kind=kOutput, calls=%fused_computation.4 | convolution fusion | flops 2147745792 | bytes 11010048 | tf_op jit(solution)/shard_map/dot_general | solution.py:96
  14.0 0.1 copy.11
  14.1 0.1 copy.9
  14.2 0.0 copy-done.3
  14.2 2.4 fusion.1
  16.6 0.0 copy-start.2
  16.7 0.1 copy.12
  16.8 0.1 copy.10
  16.9 1.1 maximum_bitcast_fusion
  17.9 0.0 all-gather.3.cloned.1.call-update
  18.0 0.0 copy-done.2
  18.0 17.6 %all_gather.11.segk_ref = s32[16,2,128]{2,1,0:T(2,128)} all-gather(s32[1,2,128]{2,1,0:T(2,128)S(1)} %bitcast.24), channel_id=1, replica_groups=mesh['dp'=2,'cp'=16] {'cp'}, dimensions={0}, use_global_device_ids=true | all-gather | bytes 17408 | tf_op jit(solution)/shard_map/all_gather | solution.py:101
  35.6 16.6 %convolution_convert_fusion.1.q_ref = bf16[256,4096]{1,0:T(8,128)(2,1)} fusion(bf16[256,4096]{1,0:T(8,128)(2,1)S(1)} %copy-done, bf16[4096,4096]{1,0:T(8,128)(2,1)} %param.8), kind=kOutput, calls=%fused_computation.1 | convolution fusion | flops 8590983168 | bytes 37748736 | tf_op jit(solution)/shard_map/dot_general | solution.py:102
  52.2 91.7 %all-gather.3.cloned.1.call-done = bf16[32,8,2,128,128]{4,3,2,1,0:T(8,128)(2,1)} async-done(((bf16[2,8,2,128,128]{4,3,2,1,0:T(8,128)(2,1)}), bf16[32,8,2,128,128]{4,3,2,1,0:T(8,128)(2,1)}) %all-gather.3.cloned.1.call-update) | async-done | bytes 16777232 | tf_op jit(solution)/shard_map/all_gather | solution.py:100
  143.9 113.0 %shard_map.64 = bf16[256,4096]{1,0:T(8,128)(2,1)} custom-call(bf16[256,4096]{1,0:T(8,128)(2,1)} %convolution_convert_fusion.1.q_ref, bf16[16,2,8,2,128,128]{5,4,3,2,1,0:T(8,128)(2,1)} %bitcast.25, s32[2,128]{1,0:T(2,128)} %bitcast.23, s32[16,2,128]{2,1,0:T(2,128)} %all_gather.11.segk_ref), custom_call_target="tpu_custom_call" | custom-call | flops 10000000000 | bytes 20000000 | tf_op jit(solution)/shard_map/pallas_call | solution.py:103
  257.0 0.0 copy-start.1
  257.0 16.8 %convolution_convert_fusion = bf16[256,4096]{1,0:T(8,128)(2,1)} fusion(bf16[256,4096]{1,0:T(8,128)(2,1)} %shard_map.64, bf16[4096,4096]{1,0:T(8,128)(2,1)} %param.11), kind=kOutput, calls=%fused_computation | convolution fusion | flops 8590983168 | bytes 37748736 | tf_op jit(solution)/shard_map/dot_general | solution.py:122
  273.7 0.0 copy-done.1
Async XLA Ops:
  6.5 1.6 copy-start
  6.5 137.4 %all-gather.3.cloned.1.call-start = ((), (), s32[]{:S(2)}) async-start(), calls=%async_computation | async-start | bytes 17825792 | tf_op jit(solution)/shard_map/all_gather | solution.py:100
  8.1 6.1 %copy-start.3 = (bf16[4096,1024]{1,0:T(8,128)(2,1)S(1)}, bf16[4096,1024]{1,0:T(8,128)(2,1)}, u32[]{:S(2)}) copy-start(bf16[4096,1024]{1,0:T(8,128)(2,1)} %param.10) | copy-start | bytes 25165828
  16.6 1.3 copy-start.2
  257.0 16.8 %copy-start.1 = (bf16[256,4096]{1,0:T(8,128)(2,1)S(1)}, bf16[256,4096]{1,0:T(8,128)(2,1)}, u32[]{:S(2)}) copy-start(bf16[256,4096]{1,0:T(8,128)(2,1)} %param.6) | copy-start | bytes 6291460
Sparse Core Ops, SparseCore 0:
  18.1 125.7 all-gather.2

commit v2 on v0

v2 whole, which is shorter than its diff:
```python
import functools
import math

import jax
import jax.numpy as jnp
from jax import lax
from jax.experimental import pallas as pl
from jax.experimental.pallas import tpu as pltpu
from jax.sharding import PartitionSpec as P

DH = 128
NKV = 8
G = 4
PIECE = 128
CH = 4 * PIECE
R = G * PIECE
D = 4096
SCALE = math.log2(math.e) / math.sqrt(DH)
NEG = -1e30
MESH = pl.DeviceIdType.MESH
NWB = 5
N_SEND = (12, 15, 20, 17)
N_RECV = ((3, 4, 6, 4), (1, 2, 4, 3), (0, 0, 0, 1), (6, 8, 12, 10))


def _dot_t(a, b):
    return lax.dot_general(a, b, (((1,), (1,)), ((), ())), preferred_element_type=jnp.float32)


def _dot(a, b):
    return lax.dot_general(a, b, (((1,), (0,)), ((), ())), preferred_element_type=jnp.float32)


def _chunk_of(z, n):
    t = n - (z + 1)
    c_lo = jnp.where(n == 0, z, n - 1)
    c_far = jnp.where(t == 0, 4, jnp.where(t <= 4, t - 1, 5))
    c_near = jnp.where(t == 1, 5, 4)
    lo = t < 0
    c = jnp.where(lo, c_lo, jnp.where(z >= 2, c_far, c_near))
    return jnp.where(lo, 0, 1), c, (z >= 2) | (t <= 1)


def _mask(out_ref, me, own, low_query, seg_ref, dev, low_key, valid=True):
    def pick(low, both):
        return jnp.where(low, both[:1], both[1:])
    def piece(low, d):
        return jnp.where(low, d, 31 - d) * PIECE
    shape = (PIECE, PIECE)
    sq = jnp.transpose(jnp.broadcast_to(pick(low_query, own), shape))
    rows = lax.broadcasted_iota(jnp.int32, shape, 0) + piece(low_query, me)
    lanes = lax.broadcasted_iota(jnp.int32, shape, 1)
    for j in range(4):
        ok = (sq == pick(low_key, seg_ref[dev + j])) & (lanes + piece(low_key, dev + j) <= rows) & valid
        out_ref[:, j * PIECE:(j + 1) * PIECE] = jnp.where(ok, 0.0, NEG)


def _fused_kernel(x_ref, seg_ref, wk_ref, wv_ref, wq_ref, wo_ref, y_ref, flag_ref,
                  kv_ref, q_ref, w_ref, s_ref, bias_ref, m_ref, l_ref, acc_ref, yacc_ref, o_ref,
                  seg_all, seg_other, ssem, rsem, wsem, seg_lsem, seg_ssem, seg_rsem, seg_osem):
    me = lax.axis_index("cp")
    dp = lax.axis_index("dp")
    z = me // 4
    y = (me // 2) % 2
    c = me % 2
    yb = 1 - y
    to_y = 4 * z + 2 * yb + c
    to_c = 4 * z + 2 * y + (1 - c)

    def tile_copies(t):
        slot = lax.rem(t, NWB)
        buf, sem = w_ref.at[slot], wsem.at[slot]
        def kv_tile():
            return [pltpu.make_async_copy(w.at[:, pl.ds(pl.multiple_of(256 * t, 256), 256)], buf.at[:, pl.ds(256 * i, 256)], sem)
                    for i, w in enumerate((wk_ref, wv_ref))]
        def q_tile():
            return [pltpu.make_async_copy(wq_ref.at[:, pl.ds(pl.multiple_of(512 * (t - 4), 512), 512)], buf, sem)]
        def o_tile():
            return [pltpu.make_async_copy(wo_ref.at[pl.ds(pl.multiple_of(512 * (t - 12), 512), 512), pl.ds(512 * j, 512)],
                                          buf.at[pl.ds(512 * j, 512), :], sem) for j in range(8)]
        return kv_tile, q_tile, o_tile

    def start_tile(t):
        kv_tile, q_tile, o_tile = tile_copies(t)
        @pl.when(t < 4)
        def _():
            for cp in kv_tile():
                cp.start()
        @pl.when((t >= 4) & (t < 12))
        def _():
            for cp in q_tile():
                cp.start()
        @pl.when((t >= 12) & (t < 20))
        def _():
            for cp in o_tile():
                cp.start()

    def wait_tile(t):
        slot = lax.rem(t, NWB)
        pltpu.make_async_copy(wq_ref.at[:, pl.ds(0, 512)], w_ref.at[slot], wsem.at[slot]).wait()

    own_seg = pltpu.make_async_copy(seg_ref, seg_all.at[me], seg_lsem)
    own_seg.start()
    for t in range(NWB):
        start_tile(jnp.int32(t))

    barrier = pltpu.get_barrier_semaphore()
    for i in range(1, 16):
        pl.semaphore_signal(barrier, inc=1, device_id={"cp": lax.rem(me + i, 16)}, device_id_type=MESH)
    pl.semaphore_signal(barrier, inc=1, device_id={"dp": 1 - dp}, device_id_type=MESH)

    def enter(_):
        pl.semaphore_wait(barrier, 16)

    def share_seg(_):
        own_seg.wait()
        for i in range(1, 16):
            pltpu.make_async_remote_copy(src_ref=seg_all.at[me], dst_ref=seg_all.at[me], send_sem=seg_ssem, recv_sem=seg_rsem,
                                         device_id={"cp": lax.rem(me + i, 16)}, device_id_type=MESH).start()

    seg_swap = pltpu.make_async_remote_copy(src_ref=seg_all, dst_ref=seg_other, send_sem=seg_osem.at[0], recv_sem=seg_osem.at[1],
                                            device_id={"dp": 1 - dp}, device_id_type=MESH)

    def low(k, yy):
        return 4 * k + 2 * yy + c
    def own_high(yy):
        return 16 + 2 * yy + c
    def up_high(yy):
        return 20 + 2 * yy + c

    def send(h, stage, target, src, dst=None):
        dst = src if dst is None else dst
        pltpu.make_async_remote_copy(src_ref=kv_ref.at[h, src], dst_ref=kv_ref.at[h, dst], send_sem=ssem.at[h],
                                     recv_sem=rsem.at[h, stage], device_id={"cp": target}, device_id_type=MESH).start()

    def mate(h, *items):
        for i in items:
            send(h, 3, to_c, i)

    def t0(h):
        @pl.when(z == 0)
        def _():
            send(h, 0, me + 12, low(0, y))
            send(h, 0, me + 8, low(0, y))
            send(h, 0, me + 4, low(0, y))
            send(h, 0, to_y, low(0, y))
            send(h, 0, to_y, own_high(y))
            mate(h, low(0, y), own_high(y))
        for zz in (1, 2):
            @pl.when(z == zz)
            def _():
                send(h, 0, me + 4, low(zz, y))
                send(h, 0, to_y, low(zz, y))
                send(h, 0, to_y, own_high(y))
                send(h, 0, me - 4, own_high(y), up_high(y))
                mate(h, low(zz, y), own_high(y))
        @pl.when(z == 3)
        def _():
            send(h, 0, me - 4, low(3, y))
            send(h, 0, to_y, low(3, y))
            send(h, 0, to_y, own_high(y))
            send(h, 0, me - 4, own_high(y), up_high(y))
            mate(h, low(3, y), own_high(y))

    def arrive(h, stage):
        for zz in range(4):
            n = N_RECV[stage][zz]
            if n:
                @pl.when(z == zz)
                def _():
                    pltpu.make_async_copy(kv_ref.at[h, pl.ds(0, n)], kv_ref.at[h, pl.ds(0, n)], rsem.at[h, stage]).wait()

    def w1(h):
        arrive(h, 0)
        @pl.when(z == 0)
        def _():
            send(h, 1, to_y, up_high(y))
            mate(h, low(0, yb), own_high(yb), up_high(y))
        @pl.when(z == 1)
        def _():
            send(h, 1, me + 4, low(1, yb))
            send(h, 1, to_y, low(0, y))
            send(h, 1, to_y, up_high(y))
            mate(h, low(1, yb), own_high(yb), low(0, y), up_high(y))
        @pl.when(z == 2)
        def _():
            send(h, 1, me + 4, low(1, y))
            send(h, 1, me + 4, low(2, yb))
            send(h, 1, to_y, low(0, y))
            send(h, 1, to_y, up_high(y))
            mate(h, low(2, yb), low(1, y), low(0, y), up_high(y), own_high(yb), low(3, y))
        @pl.when(z == 3)
        def _():
            send(h, 1, to_y, low(0, y))
            send(h, 1, me - 4, low(3, yb))
            mate(h, low(0, y), low(3, yb), own_high(yb), low(2, y))

    def w2(h):
        arrive(h, 1)
        @pl.when(z == 0)
        def _():
            mate(h, up_high(yb))
        @pl.when(z == 1)
        def _():
            mate(h, low(0, yb), up_high(yb))
        @pl.when(z == 2)
        def _():
            mate(h, low(1, yb), low(3, yb), low(0, yb), up_high(yb))
        @pl.when(z == 3)
        def _():
            send(h, 2, to_y, low(1, y))
            mate(h, low(1, y), low(2, yb), low(0, yb))

    def w3(h):
        arrive(h, 2)
        @pl.when(z == 3)
        def _():
            mate(h, low(1, yb))

    def w4(h):
        arrive(h, 3)

    def kv_step(t):
        wait_tile(t)
        r = _dot(x_ref[...], w_ref[lax.rem(t, NWB)]).astype(jnp.bfloat16)
        for sel, slot in ((0, low(z, y)), (1, own_high(y))):
            for i in range(2):
                for j in range(2):
                    kv_ref[2 * t + i, slot, j] = r[sel * PIECE:(sel + 1) * PIECE, 256 * j + 128 * i:256 * j + 128 * (i + 1)]
        start_tile(t + NWB)

    def kv_body(t, _):
        kv_step(t)
        run(kv_plan, t)
        return 0

    def run(plan, i):
        for when, *what in plan:
            @pl.when(i == when)
            def _():
                for fn, head in what:
                    fn(head)

    kv_plan = (
        (0, (enter, 0), (t0, 0), (t0, 1), (share_seg, 0)),
        (1, (t0, 2)),
        (3, (w1, 0)),
    )
    lax.fori_loop(0, 4, kv_body, 0)

    def make_bias(_):
        pltpu.make_async_copy(seg_all.at[pl.ds(0, 15)], seg_all.at[pl.ds(0, 15)], seg_rsem).wait()
        seg_swap.start()
        own = seg_all[me]
        def body(n, _):
            sel, ck, valid = _chunk_of(z, n)
            low_key = ck < 4
            dev = jnp.where(low_key, 4 * ck, jnp.minimum(4 * (z + ck - 4), 12))
            _mask(bias_ref.at[n], me, own, sel == 0, seg_all, dev, low_key, valid)
            return 0
        lax.fori_loop(0, 3 * groups, body, 0)

    groups = jnp.where(z >= 2, 3, z + 1)

    def q_body(j, _):
        t = j + 4
        wait_tile(t)
        r = _dot(x_ref[...], w_ref[lax.rem(t, NWB)]).astype(jnp.bfloat16)
        for sel in range(2):
            for g in range(G):
                q_ref[j, sel, g * PIECE:(g + 1) * PIECE, :] = r[sel * PIECE:(sel + 1) * PIECE, g * DH:(g + 1) * DH]
        start_tile(t + NWB)
        run(q_plan, j)
        return 0

    q_plan = (
        (0, (t0, 3)),
        (2, (w1, 1)),
        (3, (w2, 0), (make_bias, 0)),
        (4, (t0, 4)),
        (5, (w3, 0), (w1, 2)),
        (6, (w2, 1)),
    )

    lax.fori_loop(0, 8, q_body, 0)

    def score(h, n):
        sel, ck, _ = _chunk_of(z, n)
        k = kv_ref[h, pl.ds(4 * ck, 4), 0].reshape(CH, DH)
        s = _dot_t(q_ref[h, sel], k)
        s = (s.reshape(G, PIECE, CH) * SCALE + bias_ref[n][None]).reshape(R, CH)
        s_ref[n] = s
        s = [s[:, i * DH:(i + 1) * DH] for i in range(4)]
        m_ref[sel] = jnp.maximum(m_ref[sel], functools.reduce(jnp.maximum, s))

    def weigh(h, n):
        sel, ck, _ = _chunk_of(z, n)
        v = kv_ref[h, pl.ds(4 * ck, 4), 1].reshape(CH, DH)
        m = m_ref[sel]
        p = [jnp.exp2(s_ref[n, :, i * DH:(i + 1) * DH] - m) for i in range(4)]
        l_ref[sel] = l_ref[sel] + functools.reduce(jnp.add, p)
        pb = jnp.concatenate([a.astype(jnp.bfloat16) for a in p], axis=1)
        acc_ref[sel] = acc_ref[sel] + _dot(pb, v)

    def steps(fn, h):
        def group(i, _):
            for u in range(3):
                fn(h, 3 * i + u)
            return 0
        lax.fori_loop(0, groups, group, 0)

    def project(t, last):
        slots = lax.rem(t, NWB), lax.rem(t + 1, NWB)
        for j in range(8):
            cols = slice(R * j, R * (j + 1))
            r = _dot(o_ref[0], w_ref[slots[0], cols, :]) + _dot(o_ref[1], w_ref[slots[1], cols, :])
            if last:
                y_ref[:, cols] = (yacc_ref[:, cols] + r).astype(jnp.bfloat16)
            else:
                yacc_ref[:, cols] = yacc_ref[:, cols] + r
        start_tile(t + NWB)
        start_tile(t + 1 + NWB)

    def attend(h, half, last=False):
        def ahead(n, fn):
            @pl.when(h + n < NKV)
            def _():
                fn(h + n)
        if not last:
            ahead(5, t0)
            ahead(3, w1)
            ahead(1, w3)
        w4(h)
        m_ref[...] = jnp.full_like(m_ref, -jnp.inf)
        l_ref[...] = jnp.zeros_like(l_ref)
        acc_ref[...] = jnp.zeros_like(acc_ref)
        steps(score, h)
        if not last:
            ahead(2, w2)
        for sel in range(2):
            m_ref[sel] = jnp.broadcast_to(jnp.max(m_ref[sel], axis=1, keepdims=True), (R, DH))
        steps(weigh, h)
        t = h + 11
        if half:
            wait_tile(t)
            wait_tile(t + 1)
        for sel in range(2):
            a = (acc_ref[sel] / jnp.sum(l_ref[sel], axis=1, keepdims=True)).astype(jnp.bfloat16)
            for g in range(G):
                o_ref[half, sel * PIECE:(sel + 1) * PIECE, g * DH:(g + 1) * DH] = a[g * PIECE:(g + 1) * PIECE]
        if half:
            project(t, last)

    yacc_ref[...] = jnp.zeros_like(yacc_ref)

    def pair(i, _):
        attend(2 * i, 0)
        attend(2 * i + 1, 1)
        return 0
    lax.fori_loop(0, 3, pair, 0)
    attend(jnp.int32(6), 0)
    attend(jnp.int32(7), 1, last=True)

    seg_swap.wait()
    def reach(ref):
        def first(d):
            return jnp.broadcast_to(ref[d][1:2, 0:1], (1, PIECE))
        def last_(d):
            return jnp.broadcast_to(ref[d][1:2, PIECE - 1:PIECE], (1, PIECE))
        return (first(7) == last_(12)) | (first(3) == last_(8))
    flag_ref[...] = jnp.where(reach(seg_all) | reach(seg_other), 1, 0)

    pltpu.make_async_copy(seg_all.at[pl.ds(0, 15)], seg_all.at[pl.ds(0, 15)], seg_ssem).wait()
    def drain(h, _):
        for zz in range(4):
            @pl.when(z == zz)
            def _():
                ref = kv_ref.at[h, pl.ds(0, N_SEND[zz])]
                pltpu.make_async_copy(ref, ref, ssem.at[h]).wait()
        return 0
    lax.fori_loop(0, NKV, drain, 0)


def _fused(x, seg, wq, wk, wv, wo):
    vmem = pl.BlockSpec(memory_space=pltpu.VMEM)
    hbm = pl.BlockSpec(memory_space=pl.ANY)
    dma = pltpu.SemaphoreType.DMA
    return pl.pallas_call(
        _fused_kernel,
        out_shape=(jax.ShapeDtypeStruct((2 * PIECE, D), jnp.bfloat16), jax.ShapeDtypeStruct((1, PIECE), jnp.int32)),
        in_specs=[vmem, hbm, hbm, hbm, hbm, hbm],
        out_specs=(vmem, vmem),
        scratch_shapes=[
            pltpu.VMEM((NKV, 24, 2, PIECE, DH), jnp.bfloat16),
            pltpu.VMEM((NKV, 2, R, DH), jnp.bfloat16),
            pltpu.VMEM((NWB, D, 512), jnp.bfloat16),
            pltpu.VMEM((9, R, CH), jnp.float32),
            pltpu.VMEM((9, PIECE, CH), jnp.float32),
            pltpu.VMEM((2, R, DH), jnp.float32),
            pltpu.VMEM((2, R, DH), jnp.float32),
            pltpu.VMEM((2, R, DH), jnp.float32),
            pltpu.VMEM((2 * PIECE, D), jnp.float32),
            pltpu.VMEM((2, 2 * PIECE, R), jnp.bfloat16),
            pltpu.VMEM((16, 2, PIECE), jnp.int32),
            pltpu.VMEM((16, 2, PIECE), jnp.int32),
            dma((NKV,)),
            dma((NKV, 4)),
            dma((NWB,)),
            dma, dma, dma,
            dma((2,)),
        ],
        compiler_params=pltpu.CompilerParams(collective_id=0, has_side_effects=True, vmem_limit_bytes=67043328),
        cost_estimate=pl.CostEstimate(flops=30_000_000_000, bytes_accessed=90_000_000, transcendentals=0),
    )(x, seg.reshape(2, PIECE), wk, wv, wq, wo)


def _chunk_any(z, n):
    lo = n <= z
    t = n - (z + 1)
    c_lo = jnp.where(n == 0, z, n - 1)
    c_hi = jnp.where(t == 0, 4 + z, jnp.where(t <= 4, t - 1, z + t))
    return lo, jnp.where(lo, c_lo, c_hi)


def _any_kernel(q_ref, kv_ref, seg_ref, o_ref, bias_ref, m_ref, l_ref, acc_ref):
    me = lax.axis_index("cp")
    z = me // 4
    m_ref[...] = jnp.full_like(m_ref, -jnp.inf)
    l_ref[...] = jnp.zeros_like(l_ref)
    acc_ref[...] = jnp.zeros_like(acc_ref)
    own = seg_ref[me]

    def body(n, _):
        lo, ck = _chunk_any(z, n)
        sel = jnp.where(lo, 0, 1)
        hi = jnp.where(ck >= 4, 1, 0)
        dev0 = 4 * (ck - 4 * hi)
        _mask(bias_ref, me, own, lo, seg_ref, dev0, hi == 0)
        k = kv_ref[pl.ds(dev0, 4), hi, 0, 0].reshape(CH, DH)
        v = kv_ref[pl.ds(dev0, 4), hi, 0, 1].reshape(CH, DH)
        for g in range(G):
            i = sel * G + g
            s = _dot_t(q_ref[sel, 0, g], k) * SCALE + bias_ref[...]
            m_old = m_ref[i]
            m_new = jnp.maximum(m_old, jnp.max(s, axis=1, keepdims=True))
            p = jnp.exp2(s - m_new[:, :1])
            corr = jnp.exp2(m_old - m_new)
            l_ref[i] = l_ref[i] * corr + jnp.sum(p, axis=1, keepdims=True)
            acc_ref[i] = acc_ref[i] * corr + _dot(p.astype(jnp.bfloat16), v)
            m_ref[i] = m_new
        return 0
    lax.fori_loop(0, 9, body, 0)
    for sel in range(2):
        for g in range(G):
            o_ref[sel, 0, g] = (acc_ref[sel * G + g] / l_ref[sel * G + g]).astype(jnp.bfloat16)


def _general(x, seg, wq, wk, wv, wo, n):
    perm = [(j, (j + 1) % n) for j in range(n)]
    k = jnp.dot(x, wk, preferred_element_type=jnp.float32).astype(jnp.bfloat16)
    v = jnp.dot(x, wv, preferred_element_type=jnp.float32).astype(jnp.bfloat16)
    kv = jnp.stack([k.reshape(2, PIECE, NKV, DH), v.reshape(2, PIECE, NKV, DH)], axis=0)
    kv = jnp.transpose(kv, (1, 3, 0, 2, 4))
    seg = seg.reshape(2, PIECE)
    me = lax.axis_index("cp")

    def body(i, carry):
        kv, sg, kv_all, sg_all = carry
        src = (me - i) % n
        kv_all = lax.dynamic_update_index_in_dim(kv_all, kv, src, 0)
        sg_all = lax.dynamic_update_index_in_dim(sg_all, sg, src, 0)
        return lax.ppermute(kv, "cp", perm), lax.ppermute(sg, "cp", perm), kv_all, sg_all
    init = (kv, seg, jnp.zeros((n,) + kv.shape, kv.dtype), jnp.zeros((n,) + seg.shape, seg.dtype))
    _, _, kv_all, seg_all = lax.fori_loop(0, n, body, init)
    q = jnp.dot(x, wq, preferred_element_type=jnp.float32).astype(jnp.bfloat16)
    q = jnp.transpose(q.reshape(2, PIECE, NKV, G, DH), (0, 2, 3, 1, 4))
    o = pl.pallas_call(
        _any_kernel,
        out_shape=jax.ShapeDtypeStruct((2, NKV, G, PIECE, DH), jnp.bfloat16),
        grid=(NKV,),
        in_specs=[
            pl.BlockSpec((2, 1, G, PIECE, DH), lambda h: (0, h, 0, 0, 0)),
            pl.BlockSpec((n, 2, 1, 2, PIECE, DH), lambda h: (0, 0, h, 0, 0, 0)),
            pl.BlockSpec((n, 2, PIECE), lambda h: (0, 0, 0)),
        ],
        out_specs=pl.BlockSpec((2, 1, G, PIECE, DH), lambda h: (0, h, 0, 0, 0)),
        scratch_shapes=[pltpu.VMEM((PIECE, CH), jnp.float32)] + [pltpu.VMEM((2 * G, PIECE, DH), jnp.float32)] * 3,
    )(q, kv_all, seg_all)
    o = jnp.transpose(o, (0, 3, 1, 2, 4)).reshape(2 * PIECE, NKV * G * DH)
    return jnp.dot(o, wo, preferred_element_type=jnp.float32).astype(jnp.bfloat16)


def solution(mesh):
    n = mesh.shape["cp"]

    def local(x, seg, wq, wk, wv, wo):
        y, flag = _fused(x, seg, wq, wk, wv, wo)
        return lax.cond(flag[0, 0] > 0, lambda y: _general(x, seg, wq, wk, wv, wo, n), lambda y: y, y)

    rows = P(("dp", "cp"), None)
    return jax.shard_map(local, mesh=mesh, in_specs=(rows, P(("dp", "cp")), P(), P(), P(), P()), out_specs=rows, check_vma=False)
```

time: 475 us -> 91.5 us (0.19)
  the two profiles are of different devices: /device:TPU:5 before, /device:TPU:16 now
where the time goes in v2:
time: 91.5 us; the launch traced here: 91.3 us
  Pallas kernels  86 us (94%)
  local copies, waits for them, and re-layouts  4.38 us (5%)
    pallas_call x1, Pallas kernels, _fused(): pl.pallas_call(_fused_kernel, out_shape=(jax.ShapeDtypeStruct((2 * PIECE,...  86 us
    unnamed x2, local copies, waits for them, and re-layouts  4.38 us

profile of v2, /device:TPU:16, one launch (start us, length us, event | category | flops | bytes accessed | tf_op | source)
XLA Modules:
  0.0 91.3 jit_solution(3109094822279844665)
XLA Ops:
  0.0 1.3 %copy.40 = s32[256]{0:T(256)} copy(s32[256]{0:T(256)} %param.11) | data formatting | bytes 2048
  1.3 86.0 %shard_map.66 = (bf16[256,4096]{1,0:T(8,128)(2,1)}, s32[1,128]{1,0:T(1,128)}) custom-call(bf16[256,4096]{1,0:T(8,128)(2,1)} %x_ref.1, s32[2,128]{1,0:T(2,128)} %bitcast.38, bf16[4096,1024]{1,0:T(8,128)(2,1)} %wk_ref.1, bf16[4096,1024]{1,0:T(8,128)(2,1)} %wv_ref.1, bf16[4096,4096]{1,0:T(8,128)(2,1)} %wq_ref.1, bf16[4096,4096]{1,0:T(8,128)(2,1)} %wo_ref.1), custom_call_target="tpu_custom_call" | custom-call | flops 30000001024 | bytes 90000000 | tf_op jit(solution)/shard_map/pallas_call | solution.py:388
  87.9 0.3 conditional.1
  88.1 3.1 %copy.41 = bf16[256,4096]{1,0:T(8,128)(2,1)} copy(bf16[256,4096]{1,0:T(8,128)(2,1)} %get-tuple-element.187) | data formatting | bytes 4194304

commit v3 on v2

--- a/solution.py
+++ b/solution.py
@@ -19,8 +19,8 @@
 NEG = -1e30
 MESH = pl.DeviceIdType.MESH
 NWB = 5
-N_SEND = (12, 15, 20, 17)
-N_RECV = ((3, 4, 6, 4), (1, 2, 4, 3), (0, 0, 0, 1), (6, 8, 12, 10))
+N_SEND = (11, 15, 21, 17)
+N_RECV = ((3, 4, 6, 3), (1, 2, 4, 3), (0, 0, 0, 2), (6, 8, 12, 10))
 
 
 def _dot_t(a, b):
@@ -140,7 +140,6 @@
     def t0(h):
         @pl.when(z == 0)
         def _():
-            send(h, 0, me + 12, low(0, y))
             send(h, 0, me + 8, low(0, y))
             send(h, 0, me + 4, low(0, y))
             send(h, 0, to_y, low(0, y))
@@ -186,14 +185,14 @@
         def _():
             send(h, 1, me + 4, low(1, y))
             send(h, 1, me + 4, low(2, yb))
+            send(h, 1, me + 4, low(0, y))
             send(h, 1, to_y, low(0, y))
             send(h, 1, to_y, up_high(y))
             mate(h, low(2, yb), low(1, y), low(0, y), up_high(y), own_high(yb), low(3, y))
         @pl.when(z == 3)
         def _():
-            send(h, 1, to_y, low(0, y))
             send(h, 1, me - 4, low(3, yb))
-            mate(h, low(0, y), low(3, yb), own_high(yb), low(2, y))
+            mate(h, low(3, yb), own_high(yb), low(2, y))
 
     def w2(h):
         arrive(h, 1)
@@ -209,13 +208,14 @@
         @pl.when(z == 3)
         def _():
             send(h, 2, to_y, low(1, y))
-            mate(h, low(1, y), low(2, yb), low(0, yb))
+            send(h, 2, to_y, low(0, y))
+            mate(h, low(1, y), low(0, y), low(2, yb))
 
     def w3(h):
         arrive(h, 2)
         @pl.when(z == 3)
         def _():
-            mate(h, low(1, yb))
+            mate(h, low(0, yb), low(1, yb))
 
     def w4(h):
         arrive(h, 3)
@@ -242,8 +242,8 @@
                     fn(head)
 
     kv_plan = (
-        (0, (enter, 0), (t0, 0), (t0, 1), (share_seg, 0)),
-        (1, (t0, 2)),
+        (0, (enter, 0), (t0, 0), (share_seg, 0)),
+        (1, (t0, 1), (t0, 2)),
         (3, (w1, 0)),
     )
     lax.fori_loop(0, 4, kv_body, 0)
@@ -274,14 +274,12 @@
         return 0
 
     q_plan = (
-        (0, (t0, 3)),
-        (2, (w1, 1)),
+        (1, (w1, 1)),
+        (2, (t0, 3)),
         (3, (w2, 0), (make_bias, 0)),
-        (4, (t0, 4)),
-        (5, (w3, 0), (w1, 2)),
-        (6, (w2, 1)),
+        (4, (w1, 2)),
+        (7, (w2, 1), (w3, 0)),
     )
-
     lax.fori_loop(0, 8, q_body, 0)
 
     def score(h, n):
@@ -302,12 +300,12 @@
         pb = jnp.concatenate([a.astype(jnp.bfloat16) for a in p], axis=1)
         acc_ref[sel] = acc_ref[sel] + _dot(pb, v)
 
-    def steps(fn, h):
+    def steps(fn, h, first, last):
         def group(i, _):
             for u in range(3):
                 fn(h, 3 * i + u)
             return 0
-        lax.fori_loop(0, groups, group, 0)
+        lax.fori_loop(first, last, group, 0)
 
     def project(t, last):
         slots = lax.rem(t, NWB), lax.rem(t + 1, NWB)
@@ -326,20 +324,22 @@
             @pl.when(h + n < NKV)
             def _():
                 fn(h + n)
-        if not last:
-            ahead(5, t0)
-            ahead(3, w1)
-            ahead(1, w3)
         w4(h)
         m_ref[...] = jnp.full_like(m_ref, -jnp.inf)
         l_ref[...] = jnp.zeros_like(l_ref)
         acc_ref[...] = jnp.zeros_like(acc_ref)
-        steps(score, h)
+        steps(score, h, 0, 1)
         if not last:
-            ahead(2, w2)
+            ahead(4, t0)
+        steps(score, h, 1, groups)
+        if not last:
+            ahead(3, w1)
         for sel in range(2):
             m_ref[sel] = jnp.broadcast_to(jnp.max(m_ref[sel], axis=1, keepdims=True), (R, DH))
-        steps(weigh, h)
+        steps(weigh, h, 0, groups)
+        if not last:
+            ahead(1, w3)
+            ahead(2, w2)
         t = h + 11
         if half:
             wait_tile(t)

time: 91.5 us -> 81 us (0.89)
  the two profiles are of different devices: /device:TPU:16 before, /device:TPU:27 now
where the time goes in v3:
time: 81 us; the launch traced here: 80.8 us
  Pallas kernels  75.5 us (93%)
  local copies, waits for them, and re-layouts  4.38 us (5%)
    pallas_call x1, Pallas kernels, _fused(): pl.pallas_call(_fused_kernel, out_shape=(jax.ShapeDtypeStruct((2 * PIECE,...  75.5 us
    unnamed x2, local copies, waits for them, and re-layouts  4.38 us

profile of v3, /device:TPU:27, one launch (start us, length us, event | category | flops | bytes accessed | tf_op | source)
XLA Modules:
  0.0 80.8 jit_solution(5285071685706932571)
XLA Ops:
  0.0 1.3 %copy.40 = s32[256]{0:T(256)} copy(s32[256]{0:T(256)} %param.11) | data formatting | bytes 2048
  1.3 75.5 %shard_map.66 = (bf16[256,4096]{1,0:T(8,128)(2,1)}, s32[1,128]{1,0:T(1,128)}) custom-call(bf16[256,4096]{1,0:T(8,128)(2,1)} %x_ref.1, s32[2,128]{1,0:T(2,128)} %bitcast.38, bf16[4096,1024]{1,0:T(8,128)(2,1)} %wk_ref.1, bf16[4096,1024]{1,0:T(8,128)(2,1)} %wv_ref.1, bf16[4096,4096]{1,0:T(8,128)(2,1)} %wq_ref.1, bf16[4096,4096]{1,0:T(8,128)(2,1)} %wo_ref.1), custom_call_target="tpu_custom_call" | custom-call | flops 30000001024 | bytes 90000000 | tf_op jit(solution)/shard_map/pallas_call | solution.py:388
  77.4 0.3 conditional.1
  77.7 3.1 %copy.41 = bf16[256,4096]{1,0:T(8,128)(2,1)} copy(bf16[256,4096]{1,0:T(8,128)(2,1)} %get-tuple-element.187) | data formatting | bytes 4194304

commit v4 on v3

--- a/solution.py
+++ b/solution.py
@@ -246,6 +246,7 @@
         (1, (t0, 1), (t0, 2)),
         (3, (w1, 0)),
     )
+    yacc_ref[...] = jnp.zeros_like(yacc_ref)
     lax.fori_loop(0, 4, kv_body, 0)
 
     def make_bias(_):
@@ -351,7 +352,6 @@
         if half:
             project(t, last)
 
-    yacc_ref[...] = jnp.zeros_like(yacc_ref)
 
     def pair(i, _):
         attend(2 * i, 0)

time: 81 us -> 80.7 us (level)
  no operation moved by 1% of the time
where the time goes in v4:
time: 80.7 us; the launch traced here: 80.5 us
  Pallas kernels  75.2 us (93%)
  local copies, waits for them, and re-layouts  4.38 us (5%)
    pallas_call x1, Pallas kernels, _fused(): pl.pallas_call(_fused_kernel, out_shape=(jax.ShapeDtypeStruct((2 * PIECE,...  75.2 us
    unnamed x2, local copies, waits for them, and re-layouts  4.38 us

profile of v4, /device:TPU:27, one launch (start us, length us, event | category | flops | bytes accessed | tf_op | source)
XLA Modules:
  0.0 80.5 jit_solution(15923028502794380924)
XLA Ops:
  0.0 1.3 %copy.40 = s32[256]{0:T(256)} copy(s32[256]{0:T(256)} %param.11) | data formatting | bytes 2048
  1.3 75.2 %shard_map.66 = (bf16[256,4096]{1,0:T(8,128)(2,1)}, s32[1,128]{1,0:T(1,128)}) custom-call(bf16[256,4096]{1,0:T(8,128)(2,1)} %x_ref.1, s32[2,128]{1,0:T(2,128)} %bitcast.38, bf16[4096,1024]{1,0:T(8,128)(2,1)} %wk_ref.1, bf16[4096,1024]{1,0:T(8,128)(2,1)} %wv_ref.1, bf16[4096,4096]{1,0:T(8,128)(2,1)} %wq_ref.1, bf16[4096,4096]{1,0:T(8,128)(2,1)} %wo_ref.1), custom_call_target="tpu_custom_call" | custom-call | flops 30000001024 | bytes 90000000 | tf_op jit(solution)/shard_map/pallas_call | solution.py:388
  77.1 0.3 conditional.1
  77.4 3.1 %copy.41 = bf16[256,4096]{1,0:T(8,128)(2,1)} copy(bf16[256,4096]{1,0:T(8,128)(2,1)} %get-tuple-element.187) | data formatting | bytes 4194304
